TPU v7x, 256 devices: a whole 4x4x8 slice. The times are simulated.
256 devices in a mesh: lon: 64 (over y, z, core), lev: 4 (over x).
Axes of the slice: x: 4, y: 4, z: 8, core: 2. Of those that a mesh axis runs over, the one named last changes fastest.
Arguments:
- column_old: float32 [70, 2097152], P(None, ('lon', 'lev')), may hold values from -6 to 6
- coupling: float32 [69, 2097152], P(None, ('lon', 'lev')), may hold values from 7.5 to 120, as said below
- sea_temp: float32 [2097152], P(('lon', 'lev')), may hold values from -6 to 6
- land_mask: int32 [2097152], P(('lon', 'lev')), may hold values from 0 to 1, as said below
- tile_weight: float32 [9, 2097152], P(None, ('lon', 'lev')), may hold values from 0.05 to 1
- tile_coeff: float32 [9, 2097152], P(None, ('lon', 'lev')), may hold values from 0.2 to 5
- tile_capacity: float32 [9, 2097152], P(None, ('lon', 'lev')), may hold values from 0.5 to 5
- tile_conduct: float32 [9, 2097152], P(None, ('lon', 'lev')), may hold values from 0.1 to 2
- tile_old: float32 [9, 2097152], P(None, ('lon', 'lev')), may hold values from -6 to 6
- tile_forcing: float32 [9, 2097152], P(None, ('lon', 'lev')), may hold values from -12 to 12
Outputs:
- column_temp: float32 [70, 2097152], P(None, ('lon', 'lev'))
- tile_temp: float32 [9, 2097152], P(None, ('lon', 'lev'))
Inputs may be any that keep to these rules, and one draw needn't show every extreme that they name: `land_mask`: 1 marks a land column, 0 an ocean column. `coupling`: positive.
All inputs are finite; a program needn't handle non-finite values.
Results may differ from a plain program's by a relative error of at most 0.0001.
Values sent between devices are 32-bit elements; how exact they have to be, the bound alone decides.
A program may use at most 64 MiB of HBM per device.

v0:
```python
import jax
import jax.numpy as jnp
from jax import lax
from jax.sharding import PartitionSpec as P

ITERS = 8


HIGH = lax.Precision.HIGHEST


def extended(value, sides, width):
    edges = {}
    for axis, dim in sides:
        size, length = (lax.axis_size(axis), value.shape[dim])
        up = [(i, (i + 1) % size) for i in range(size)]
        last = lax.slice_in_dim(value, length - width, length, axis=dim)
        leading = lax.slice_in_dim(value, 0, width, axis=dim)
        edges[dim] = (
            lax.ppermute(last, axis, up),
            lax.ppermute(leading, axis, [(b, a) for a, b in up]),
        )
    done = []
    for _, dim in sides:
        low, high = edges[dim]
        around = [(width, width) if d in done else (0, 0) for d in range(value.ndim)]
        value = jnp.concatenate([jnp.pad(low, around), value, jnp.pad(high, around)], axis=dim)
        done.append(dim)
    return value


def eliminate_upper(column_old, smooth):
    zero_row = jnp.zeros_like(smooth[:1])
    k_below = smooth[1:]
    k_above = jnp.concatenate([smooth[2:], zero_row], axis=0)

    def eliminate_one_level(carried, layer_data):
        offset_next, factor_next = carried
        right_side, below_k, above_k = layer_data
        pivots = 1.0 + below_k + above_k - above_k * factor_next
        offset = (right_side + above_k * offset_next) / pivots
        factor = below_k / pivots
        return ((offset, factor), (offset, factor))

    initial = (jnp.zeros_like(column_old[0]), jnp.zeros_like(column_old[0]))
    last, stacked = lax.scan(
        eliminate_one_level, initial, (column_old[2:], k_below, k_above), reverse=True, unroll=4
    )
    return (last[0], last[1], stacked[0], stacked[1])


def lower_levels(column_old, smooth, offset_two, factor_two, surface_flux):
    k_ground = smooth[0] * (1.0 + 0.5 * jnp.tanh(surface_flux))
    k_second = smooth[1]
    pivot_one = 1.0 + k_ground + k_second - k_second * factor_two
    offset_one = (column_old[1] + k_second * offset_two) / pivot_one
    factor_one = k_ground / pivot_one
    pivot_ground = 1.0 + k_ground - k_ground * factor_one
    return (
        (column_old[0] + k_ground * offset_one) / pivot_ground,
        1.0 / pivot_ground,
        offset_one,
        factor_one,
    )


def surface_solve(p_surf, q_surf, column_a, column_b):
    return (p_surf + q_surf * column_a) / (1.0 + q_surf * column_b)


def tile_sums(tile_weight, tile_coeff, tile_capacity, tile_conduct, tile_old, tile_forcing):
    fraction = tile_weight / jnp.sum(tile_weight, axis=0)
    denominator = tile_capacity + tile_coeff + tile_conduct
    source = tile_capacity * tile_old + tile_forcing
    land_a = jnp.sum(fraction * tile_coeff * source / denominator, axis=0)
    land_b = jnp.sum(fraction * tile_coeff * (tile_capacity + tile_conduct) / denominator, axis=0)
    return (land_a, land_b, denominator, source)


def substitute(surface, offset_one, factor_one, upper_offset, upper_factor):
    level_one = offset_one + factor_one * surface

    def substitute_one_level(below_value, layer_data):
        value = layer_data[0] + layer_data[1] * below_value
        return (value, value)

    unused, higher = lax.scan(
        substitute_one_level, level_one, (upper_offset, upper_factor), unroll=4
    )
    return jnp.concatenate([surface[None], level_one[None], higher], axis=0)


def build_tables(land_mask):
    columns = land_mask.shape[0]
    tile_count = columns // 128
    mask_tiles = land_mask.reshape(tile_count, 128).astype(jnp.float32)
    within = jnp.arange(128, dtype=jnp.int32)
    upper_ones = (within[:, None] <= within[None, :]).astype(jnp.float32)
    running = jnp.dot(mask_tiles, upper_ones, precision=HIGH, preferred_element_type=jnp.float32)
    tile_ids = jnp.arange(tile_count, dtype=jnp.int32)
    lower_ones = (tile_ids[None, :] < tile_ids[:, None]).astype(jnp.float32)
    offsets = jnp.dot(
        lower_ones, running[:, -1], precision=HIGH, preferred_element_type=jnp.float32
    )
    offsets_int = offsets.astype(jnp.int32)
    ranks = offsets_int[:, None] + running.astype(jnp.int32) - 1
    base_tile = offsets_int // 128
    local_place = ranks - base_tile[:, None] * 128
    window = jnp.arange(256, dtype=jnp.int32)
    selector = (
        (local_place[:, :, None] == window[None, None, :])
        & (land_mask.reshape(tile_count, 128)[:, :, None] == 1)
    ).astype(jnp.float32)
    first_half = (base_tile[None, :] == tile_ids[:, None]).astype(jnp.float32)
    second_half = (base_tile[None, :] + 1 == tile_ids[:, None]).astype(jnp.float32)
    return (selector, first_half, second_half)


def pack_rows(values, tables):
    selector, first_half, second_half = tables
    count = values.shape[0]
    tile_count = selector.shape[0]
    pieces = jnp.einsum(
        "mti,tio->mto",
        values.reshape(count, tile_count, 128),
        selector,
        precision=HIGH,
        preferred_element_type=jnp.float32,
    )
    placed = jnp.einsum(
        "jt,mtk->mjk",
        first_half,
        pieces[:, :, :128],
        precision=HIGH,
        preferred_element_type=jnp.float32,
    )
    placed = placed + jnp.einsum(
        "jt,mtk->mjk",
        second_half,
        pieces[:, :, 128:],
        precision=HIGH,
        preferred_element_type=jnp.float32,
    )
    return placed.reshape(count, tile_count * 128)


def unpack_rows(buffers, tables):
    selector, first_half, second_half = tables
    count = buffers.shape[0]
    tile_count = selector.shape[0]
    tiled = buffers.reshape(count, tile_count, 128)
    lower_part = jnp.einsum(
        "jt,mjk->mtk", first_half, tiled, precision=HIGH, preferred_element_type=jnp.float32
    )
    upper_part = jnp.einsum(
        "jt,mjk->mtk", second_half, tiled, precision=HIGH, preferred_element_type=jnp.float32
    )
    windows = jnp.concatenate([lower_part, upper_part], axis=2)
    picked = jnp.einsum(
        "mto,tio->mti", windows, selector, precision=HIGH, preferred_element_type=jnp.float32
    )
    return picked.reshape(count, tile_count * 128)


def on_device(
    column_old,
    coupling,
    sea_temp,
    land_mask,
    tile_weight,
    tile_coeff,
    tile_capacity,
    tile_conduct,
    tile_old,
    tile_forcing,
):
    columns = column_old.shape[1]
    peer_count = lax.axis_size("lon")
    slot_count = columns // peer_count
    rimmed = extended(coupling, ((("lon", "lev"), 1),), 1)
    smooth = (rimmed[:, :-2] + 2.0 * rimmed[:, 1:-1] + rimmed[:, 2:]) * 0.25
    offset_two, factor_two, upper_offset, upper_factor = eliminate_upper(column_old, smooth)
    land_a, land_b, denominator, source = tile_sums(
        tile_weight, tile_coeff, tile_capacity, tile_conduct, tile_old, tile_forcing
    )
    is_land = land_mask == 1
    tables = build_tables(land_mask)
    surface_flux = jnp.zeros_like(sea_temp)
    surface = jnp.zeros_like(sea_temp)
    offset_one = jnp.zeros_like(sea_temp)
    factor_one = jnp.zeros_like(sea_temp)
    remote_a, remote_b = (
        lax.all_to_all(land_a.reshape(columns, 1), "lon", split_axis=0, concat_axis=1, tiled=True),
        lax.all_to_all(land_b.reshape(columns, 1), "lon", split_axis=0, concat_axis=1, tiled=True),
    )
    unpacked = unpack_rows(
        jnp.stack([remote_a.reshape(columns), remote_b.reshape(columns)]), tables
    )
    column_a = jnp.where(is_land, unpacked[0], sea_temp)
    column_b = jnp.where(is_land, unpacked[1], jnp.ones_like(sea_temp))
    for repeat in range(ITERS):
        p_surf, q_surf, offset_one, factor_one = lower_levels(
            column_old, smooth, offset_two, factor_two, surface_flux
        )
        surface = surface_solve(p_surf, q_surf, column_a, column_b)
        surface_flux = column_a - column_b * surface
    packed = pack_rows(surface[None], tables)
    returned = lax.all_to_all(
        packed[0].reshape(slot_count, peer_count), "lon", split_axis=1, concat_axis=0, tiled=True
    )
    land_surface = returned.reshape(columns)
    tile_temp = (source + tile_coeff * land_surface) / denominator
    column_temp = substitute(surface, offset_one, factor_one, upper_offset, upper_factor)
    return (column_temp, tile_temp)


def solution(mesh):
    in_specs = (
        P(None, ("lon", "lev")),
        P(None, ("lon", "lev")),
        P(("lon", "lev")),
        P(("lon", "lev")),
        P(None, ("lon", "lev")),
        P(None, ("lon", "lev")),
        P(None, ("lon", "lev")),
        P(None, ("lon", "lev")),
        P(None, ("lon", "lev")),
        P(None, ("lon", "lev")),
    )
    out_specs = (P(None, ("lon", "lev")), P(None, ("lon", "lev")))
    return jax.shard_map(
        on_device, mesh=mesh, in_specs=in_specs, out_specs=out_specs, check_vma=False
    )
```

profile of v0, /device:TPU:1, one launch (start us, length us, event | category | flops | bytes accessed | tf_op | source)
XLA Modules:
  0.0 213.7 jit_solution(14533294864789574689)
XLA Ops:
  1.5 3.9 %collective-permute-start.1 = (f32[69,1]{1,0:T(8,128)S(1)}, f32[69,1]{1,0:T(8,128)S(1)}, u32[]{:S(2)}, u32[]{:S(2)}) collective-permute-start(f32[69,1]{1,0:T(8,128)S(1)} %get-tuple-element.303), channel_id=1, source_target_pairs={{1,0},{2,1},{3,2},{4,3},{5,4},{6,5},{7,6},{8,7},{9,8},{10,9},{11,1... | collective-permute-start | bytes 836 | tf_op jit(solution)/shard_map/ppermute | solution.py:21
  6.5 2.8 %fusion.28 = (f32[8192]{0:T(1024)}, f32[8192]{0:T(1024)}) fusion(f32[9,8192]{1,0:T(8,128)} %param.20, f32[9,8192]{1,0:T(8,128)} %param.21, f32[9,8192]{1,0:T(8,128)} %param.19, f32[9,8192]{1,0:T(8,128)} %param.18, f32[8192]{0:T(1024)S(1)} %reduce_sum.27, f32[9,8192]{1,0:T(8,128)} %param.23, f32[9,8192]{1,0:T(8,128)} %param.22), kind=kLoop, calls=%fused_computation.74 | loop fusion | flops 942080 | bytes 1867776 | tf_op jit(solution)/shard_map/reduce_sum | solution.py:76
  9.4 11.8 %all-to-all-start = ((f32[64,128,1]{1,2,0:T(1,128)}), f32[64,128,1]{1,2,0:T(1,128)S(1)}, u32[]{:S(2)}, u32[]{:S(2)}) async-start(f32[64,128,1]{1,2,0:T(1,128)} %bitcast.20), calls=%async_computation | async-start | bytes 65536 | tf_op jit(solution)/shard_map/all_to_all | solution.py:193
  22.9 1.9 slice.243
  24.8 2.0 reshape.118
  26.8 4.4 %fusion.20 = f32[69,8192]{1,0:T(8,128)S(1)} fusion(f32[69,1]{1,0:T(8,128)S(1)} %collective-permute-done.1, f32[69,8192]{1,0:T(8,128)} %param.15, f32[69,1]{1,0:T(8,128)S(1)} %collective-permute-done), kind=kLoop, calls=%fused_computation.55 | loop fusion | flops 3391488 | bytes 4522536 | tf_op jit(solution)/shard_map/mul | solution.py:181
  31.4 1.6 slice.266
  33.0 1.6 concatenate.41
  34.6 3.4 %reshape.119 = f32[17,4,8192]{2,1,0:T(4,128)} reshape(f32[68,8192]{1,0:T(8,128)} %concatenate.41) | data formatting | bytes 4456448 | tf_op jit(solution)/shard_map/reshape | solution.py:46
  38.0 3.4 %reshape.120 = f32[17,4,8192]{2,1,0:T(4,128)} reshape(f32[68,8192]{1,0:T(8,128)} %slice.266) | data formatting | bytes 4456448 | tf_op jit(solution)/shard_map/reshape | solution.py:46
  41.4 1.8 broadcast.55.clone
  43.2 1.8 broadcast.55.clone.1
  45.0 84.1 %while.34 = (s32[]{:T(128)}, f32[8192]{0:T(1024)S(1)}, f32[8192]{0:T(1024)S(1)}, f32[17,4,8192]{2,1,0:T(4,128)}, f32[17,4,8192]{2,1,0:T(4,128)}, /*index=5*/f32[...) while((s32[]{:T(128)}, f32[8192]{0:T(1024)S(1)}, ...), condition=%wide.region_4.5_spmd.clone, body=%wide.region_3.4_spmd.clone.sunk | while | flops 614407 | bytes 2490620 | solution.py:46
  47.5 1.4 constant_dynamic-slice_fusion.27
  70.9 1.3 constant_dynamic-slice_fusion.26
  75.9 1.4 constant_dynamic-slice_fusion.26
  82.1 1.5 constant_dynamic-slice_fusion.27
  89.7 1.4 constant_dynamic-slice_fusion.25
  95.9 1.4 constant_dynamic-slice_fusion.26
  114.3 1.4 constant_dynamic-slice_fusion.25
  129.1 10.3 %all-to-all-start.1 = ((f32[64,128,1]{1,2,0:T(1,128)}), f32[64,128,1]{1,2,0:T(1,128)S(1)}, u32[]{:S(2)}, u32[]{:S(2)}) async-start(f32[64,128,1]{1,2,0:T(1,128)} %bitcast.23), calls=%async_computation.1 | async-start | bytes 65536 | tf_op jit(solution)/shard_map/all_to_all | solution.py:194
  139.7 9.1 %all-to-all-done.1 = f32[64,128,1]{1,2,0:T(1,128)S(1)} async-done(((f32[64,128,1]{1,2,0:T(1,128)}), f32[64,128,1]{1,2,0:T(1,128)S(1)}, u32[]{:S(2)}, u32[]{:S(2)}) %all-to-all-start.1) | async-done | bytes 32800 | tf_op jit(solution)/shard_map/all_to_all | solution.py:194
  149.4 5.8 %fusion.22 = f32[2,64,128]{2,0,1:T(2,128)S(1)} fusion(s32[64,128]{1,0:T(8,128)S(1)} %add_subtract_fusion.1, pred[64,128]{1,0:T(8,128)(4,1)S(1)} %fusion.62, f32[2,64,256]{2,1,0:T(8,128)S(1)} %pad_maximum_fusion.3), kind=kOutput, calls=%fused_computation.59 | convolution fusion | flops 54525952 | bytes 237568 | tf_op jit(solution)/shard_map/mto,tio->mti/dot_general | solution.py:159
  156.2 31.1 %while.33 = (s32[]{:T(128)}, f32[8192]{0:T(1024)S(1)}, f32[17,4,8192]{2,1,0:T(4,128)S(1)}, f32[17,4,8192]{2,1,0:T(4,128)}, f32[17,4,8192]{2,1,0:T(4,128)}, /*index=5*/s32[]{:T(128)}, s32[]{:T(128)}, s32[]{}, s32[]{}, s32[]{}) while((s32[]{:T(128)}, f32[8192]{0:T(1024)S(1)}, f32[17,4,8192]{2,1,0:T(4,128)S(1)}, f32[17,4,8192]{2,1,0:T(4,128)}, ...), condition=%wide.region_6.7_spmd, body=%wide.region_5.6_spmd.sunk | while | flops 163845 | bytes 1212581 | solution.py:87
  156.2 1.6 constant_dynamic-slice_fusion.24
  158.0 1.5 constant_dynamic-slice_fusion.24
  159.8 1.6 constant_dynamic-slice_fusion.24
  161.6 1.6 constant_dynamic-slice_fusion.24
  163.4 1.6 constant_dynamic-slice_fusion.24
  165.2 1.6 constant_dynamic-slice_fusion.24
  167.0 1.6 constant_dynamic-slice_fusion.24
  168.8 1.6 constant_dynamic-slice_fusion.24
  170.7 1.7 constant_dynamic-slice_fusion.24
  172.5 1.6 constant_dynamic-slice_fusion.24
  174.4 1.8 constant_dynamic-slice_fusion.24
  176.3 1.6 constant_dynamic-slice_fusion.24
  178.1 1.7 constant_dynamic-slice_fusion.24
  180.1 1.6 constant_dynamic-slice_fusion.24
  181.9 1.6 constant_dynamic-slice_fusion.24
  183.7 1.5 constant_dynamic-slice_fusion.24
  185.4 1.6 constant_dynamic-slice_fusion.24
  187.2 1.4 copy-done
  188.6 2.6 %reshape.121 = f32[68,8192]{1,0:T(8,128)S(1)} reshape(f32[17,4,8192]{2,1,0:T(4,128)} %copy-done) | data formatting | bytes 4456448 | tf_op jit(solution)/shard_map/reshape | solution.py:87
  191.2 4.8 %fusion.11 = f32[64,1,256]{2,1,0:T(1,128)S(1)} fusion(f32[64,128,1]{1,2,0:T(1,128)S(1)} %bitcast.234, s32[64,128]{1,0:T(8,128)S(1)} %add_subtract_fusion.1, pred[64,128]{1,0:T(8,128)(4,1)S(1)} %fusion.62), kind=kOutput, calls=%fused_computation.47 | convolution fusion | flops 29360128 | bytes 139264 | tf_op jit(solution)/shard_map/mti,tio->mto/dot_general | solution.py:123
  197.3 4.7 %all-to-all-start.2 = ((f32[128,64,1]{0,2,1:T(1,128)}), f32[128,64,1]{0,2,1:T(1,128)S(1)}, u32[]{:S(2)}, u32[]{:S(2)}) async-start(f32[128,64,1]{0,2,1:T(1,128)} %copy.20), calls=%async_computation.2 | async-start | bytes 65536 | tf_op jit(solution)/shard_map/all_to_all | solution.py:208
  202.0 1.7 pad_maximum_fusion.2
  203.7 7.6 %all-to-all-done.2 = f32[128,64,1]{0,2,1:T(1,128)S(1)} async-done(((f32[128,64,1]{0,2,1:T(1,128)}), f32[128,64,1]{0,2,1:T(1,128)S(1)}, u32[]{:S(2)}, u32[]{:S(2)}) %all-to-all-start.2) | async-done | bytes 32800 | tf_op jit(solution)/shard_map/all_to_all | solution.py:208
  211.4 2.3 %add_divide_fusion.3 = f32[9,8192]{1,0:T(8,128)} fusion(f32[9,8192]{1,0:T(8,128)} %param.19, f32[8192]{0:T(1024)S(1)} %bitcast.236, f32[9,8192]{1,0:T(8,128)S(1)} %copy-done.2, f32[9,8192]{1,0:T(8,128)S(1)} %copy-done.1, f32[9,8192]{1,0:T(8,128)} %param.23, f32[9,8192]{1,0:T(8,128)} %param.22), kind=kLoop, calls=%fused_computation.67 | loop fusion | flops 516096 | bytes 1802240 | tf_op jit(solution)/shard_map/div | solution.py:212
  (191 shorter events, 84.2 us)
Async XLA Ops:
  0.6 20.5 %copy-start.3 = (s32[8192]{0:T(1024)S(1)}, s32[8192]{0:T(1024)}, u32[]{:S(2)}) copy-start(s32[8192]{0:T(1024)} %param.17) | copy-start | bytes 98308
  1.5 25.3 %collective-permute-start.1 = (f32[69,1]{1,0:T(8,128)S(1)}, f32[69,1]{1,0:T(8,128)S(1)}, u32[]{:S(2)}, u32[]{:S(2)}) collective-permute-start(f32[69,1]{1,0:T(8,128)S(1)} %get-tuple-element.303), channel_id=1, source_target_pairs={{1,0},{2,1},{3,2},{4,3},{5,4},{6,5},{7,6},{8,7},{9,8},{10,9},{11,1... | collective-permute-start | bytes 836 | tf_op jit(solution)/shard_map/ppermute | solution.py:21
  5.4 21.4 %collective-permute-start = (f32[69,1]{1,0:T(8,128)S(1)}, f32[69,1]{1,0:T(8,128)S(1)}, u32[]{:S(2)}, u32[]{:S(2)}) collective-permute-start(f32[69,1]{1,0:T(8,128)S(1)} %get-tuple-element.302), channel_id=1, source_target_pairs={{0,1},{1,2},{2,3},{3,4},{4,5},{5,6},{6,7},{7,8},{8,9},{9,10},{10,1... | collective-permute-start | bytes 836 | tf_op jit(solution)/shard_map/ppermute | solution.py:20
  9.4 119.8 %all-to-all-start = ((f32[64,128,1]{1,2,0:T(1,128)}), f32[64,128,1]{1,2,0:T(1,128)S(1)}, u32[]{:S(2)}, u32[]{:S(2)}) async-start(f32[64,128,1]{1,2,0:T(1,128)} %bitcast.20), calls=%async_computation | async-start | bytes 65536 | tf_op jit(solution)/shard_map/all_to_all | solution.py:193
  129.1 19.6 %all-to-all-start.1 = ((f32[64,128,1]{1,2,0:T(1,128)}), f32[64,128,1]{1,2,0:T(1,128)S(1)}, u32[]{:S(2)}, u32[]{:S(2)}) async-start(f32[64,128,1]{1,2,0:T(1,128)} %bitcast.23), calls=%async_computation.1 | async-start | bytes 65536 | tf_op jit(solution)/shard_map/all_to_all | solution.py:194
  149.4 5.9 %copy-start.4 = (f32[8192]{0:T(1024)S(1)}, f32[8192]{0:T(1024)}, u32[]{:S(2)}) copy-start(f32[8192]{0:T(1024)} %param.16) | copy-start | bytes 98308
  187.2 1.4 copy-start
  197.3 14.1 %all-to-all-start.2 = ((f32[128,64,1]{0,2,1:T(1,128)}), f32[128,64,1]{0,2,1:T(1,128)S(1)}, u32[]{:S(2)}, u32[]{:S(2)}) async-start(f32[128,64,1]{0,2,1:T(1,128)} %copy.20), calls=%async_computation.2 | async-start | bytes 65536 | tf_op jit(solution)/shard_map/all_to_all | solution.py:208
  202.0 9.4 %copy-start.1 = (f32[9,8192]{1,0:T(8,128)S(1)}, f32[9,8192]{1,0:T(8,128)}, u32[]{:S(2)}) copy-start(f32[9,8192]{1,0:T(8,128)} %param.20) | copy-start | bytes 884740
  202.0 9.3 %copy-start.2 = (f32[9,8192]{1,0:T(8,128)S(1)}, f32[9,8192]{1,0:T(8,128)}, u32[]{:S(2)}) copy-start(f32[9,8192]{1,0:T(8,128)} %param.21) | copy-start | bytes 884740
where the time goes:
time: 218 us; the launch traced here: 214 us
  local copies, waits for them, and re-layouts  118 us (54%)
  other arithmetic  34.1 us (16%)
  starting transfers between devices  30.7 us (14%)
  waiting for transfers between devices  16.7 us (8%)
  matrix products  11.9 us (5%)
    slice x51, local copies, waits for them, and re-layouts, eliminate_upper(): lax.scan(eliminate_one_level, initial, (column_old[2:], k_below, k_above)...  65.4 us
    slice x17, local copies, waits for them, and re-layouts, substitute(): lax.scan(substitute_one_level, level_one, (upper_offset, upper_factor), u...  27.6 us
    dynamic_update_slice x34, other arithmetic, eliminate_upper(): lax.scan(eliminate_one_level, initial, (column_old[2:], k_below, k_above)...  18.8 us
    all_to_all x1, starting transfers between devices, on_device(): lax.all_to_all(land_a.reshape(columns, 1), 'lon', split_axis=0, concat_ax...  11.8 us
    all_to_all x1, starting transfers between devices, on_device(): lax.all_to_all(land_b.reshape(columns, 1), 'lon', split_axis=0, concat_ax...  10.3 us
    all_to_all x1, waiting for transfers between devices, on_device(): lax.all_to_all(land_b.reshape(columns, 1), 'lon', split_axis=0, concat_ax...  9.06 us
    reshape x3, local copies, waits for them, and re-layouts, eliminate_upper(): lax.scan(eliminate_one_level, initial, (column_old[2:], k_below, k_above)...  8.82 us
    all_to_all x1, waiting for transfers between devices, on_device(): lax.all_to_all(packed[0].reshape(slot_count, peer_count), 'lon', split_ax...  7.65 us
  transfers between devices with their start and end apart: 5, of which 2 were waited for; matrix products, arithmetic and copies ran while one was open for 53% of the time, Pallas kernels for 0%

commit v1 on v0

v1 whole, which is shorter than its diff:
```python
import jax
import jax.numpy as jnp
from jax import lax
from jax.experimental import pallas as pl
from jax.experimental.pallas import tpu as pltpu
from jax.sharding import PartitionSpec as P

LEV = 70
NT = 9
COLS = 8192
ROWS = 64
LANES = 128
ITERS = 8
N_LON = 64
N_LEV = 4
MESH = pl.DeviceIdType.MESH
F32 = jnp.float32
BF16 = jnp.bfloat16
I32 = jnp.int32


def row(ref, level, start=0):
    return ref[pl.ds(level, 1), pl.ds(start, COLS)].reshape(ROWS, LANES)


def three_parts(value):
    high = value.astype(BF16)
    rest = value - high.astype(F32)
    middle = rest.astype(BF16)
    low = (rest - middle.astype(F32)).astype(BF16)
    return high, middle, low


def take(value, index):
    return jnp.take_along_axis(value, index, axis=1, mode="promise_in_bounds")


def flag(condition):
    return jnp.where(condition, 1.0, 0.0).astype(BF16)


def iota(shape, dim):
    return lax.broadcasted_iota(I32, shape, dim)


def peer_at(step, lon, sign=1):
    kz, ky, same_core = step // 8, (step // 2) % 4, step % 2
    dz = 4 + (kz // 2) * (1 - kz % 2) - ((kz + 1) // 2) * (kz % 2)
    dy = 2 + (ky // 2) * (1 - ky % 2) - ((ky + 1) // 2) * (ky % 2)
    y, z, core = lon // 16, (lon // 2) % 8, lon % 2
    return ((y + 4 + sign * dy) % 4) * 16 + ((z + 8 + sign * dz) % 8) * 2 + (core + 1 - same_core) % 2


def exchange(send, recv, send_sem, recv_sem, lon, lev):
    def copy(step, peer, landing):
        return pltpu.make_async_remote_copy(
            src_ref=send.at[pl.ds(peer, 1), :], dst_ref=recv.at[pl.ds(landing, 1), :],
            send_sem=send_sem.at[step], recv_sem=recv_sem.at[step],
            device_id={"lon": peer, "lev": lev}, device_id_type=MESH,
        )

    def start_one(step, carry):
        copy(step, peer_at(step, lon), lon).start()
        return carry

    def arrive_one(step, carry):
        copy(step, peer_at(step, lon), peer_at(step, lon, -1)).wait_recv()
        return carry

    def leave_one(step, carry):
        copy(step, peer_at(step, lon), lon).wait_send()
        return carry

    def loop(body):
        lax.fori_loop(0, N_LON - 1, body, 0, unroll=7)

    return lambda: loop(start_one), lambda: loop(arrive_one), lambda: loop(leave_one)


def kernel(
    col_h, cpl_h, sea_h, mask_h, w_h, co_h, ca_h, cd_h, old_h, fo_h,
    out_h, tile_h,
    col, cpl, es, fs, sea_s, mask_s, w_s, co_s, ca_s, cd_s, old_s, fo_s,
    scaled, coeff_r, tile_o, ab_send, ab_recv, back_send, back_recv,
    in_sem, halo_send_sem, halo_recv_sem, ab_send_sem, ab_recv_sem, back_send_sem, back_recv_sem,
    out_sem,
):
    lon, lev = lax.axis_index("lon"), lax.axis_index("lev")
    block = lon * N_LEV + lev
    right, left = (block + 1) % (N_LON * N_LEV), (block + N_LON * N_LEV - 1) % (N_LON * N_LEV)
    right_id = {"lon": right // N_LEV, "lev": right % N_LEV}
    left_id = {"lon": left // N_LEV, "lev": left % N_LEV}

    barrier = pltpu.get_barrier_semaphore()

    def greet(step, carry):
        pl.semaphore_signal(barrier, inc=1, device_id={"lon": peer_at(step, lon), "lev": lev}, device_id_type=MESH)
        return carry

    lax.fori_loop(0, N_LON - 1, greet, 0)
    for one in (left_id, right_id):
        pl.semaphore_signal(barrier, inc=1, device_id=one, device_id_type=MESH)

    own = cpl.at[:, pl.ds(LANES, COLS)]
    pairs = [
        (mask_h, mask_s), (w_h, w_s), (co_h, co_s), (ca_h, ca_s), (cd_h, cd_s), (old_h, old_s), (fo_h, fo_s),
        (cpl_h, own), (col_h, col), (sea_h, sea_s),
    ]
    loads = [pltpu.make_async_copy(src, dst, in_sem.at[n]) for n, (src, dst) in enumerate(pairs)]
    for load in loads:
        load.start()
    for load in loads[:7]:
        load.wait()

    weight_sum = sum_a = sum_b = None
    for tile in range(NT):
        weight, coeff = row(w_s, tile), row(co_s, tile)
        capacity, conduct = row(ca_s, tile), row(cd_s, tile)
        held = capacity + conduct
        inverse = 1.0 / (capacity + coeff + conduct)
        source = capacity * row(old_s, tile) + row(fo_s, tile)
        ratio = coeff * inverse
        scaled[tile] = source * inverse
        coeff_r[tile] = ratio
        share = weight * ratio
        weight_sum = weight if tile == 0 else weight_sum + weight
        sum_a = share * source if tile == 0 else sum_a + share * source
        sum_b = share * held if tile == 0 else sum_b + share * held
    whole = 1.0 / weight_sum
    ab_send[:, pl.ds(0, LANES)] = sum_a * whole
    ab_send[:, pl.ds(LANES, LANES)] = sum_b * whole
    loads[7].wait()

    pl.semaphore_wait(barrier, N_LON + 1)

    start_ab, arrive_ab, leave_ab = exchange(ab_send, ab_recv, ab_send_sem, ab_recv_sem, lon, lev)
    start_ab()
    halos = [
        pltpu.make_async_remote_copy(
            src_ref=cpl.at[:, pl.ds(COLS, LANES)], dst_ref=cpl.at[:, pl.ds(0, LANES)],
            send_sem=halo_send_sem.at[0], recv_sem=halo_recv_sem.at[0], device_id=right_id, device_id_type=MESH,
        ),
        pltpu.make_async_remote_copy(
            src_ref=cpl.at[:, pl.ds(LANES, LANES)], dst_ref=cpl.at[:, pl.ds(COLS + LANES, LANES)],
            send_sem=halo_send_sem.at[1], recv_sem=halo_recv_sem.at[1], device_id=left_id, device_id_type=MESH,
        ),
    ]
    for halo in halos:
        halo.start()
    ab_recv[pl.ds(lon, 1), :] = ab_send[pl.ds(lon, 1), :]

    lane = iota((ROWS, LANES), 1)
    is_land = mask_s[...] == 1
    land = flag(is_land)
    running = jnp.dot(land, flag(iota((LANES, LANES), 0) <= iota((LANES, LANES), 1)), preferred_element_type=F32)
    count = jnp.dot(land, jnp.ones((LANES, LANES), BF16), preferred_element_type=F32)
    before = jnp.dot(
        flag(iota((ROWS, ROWS), 1) < iota((ROWS, ROWS), 0)), count.astype(BF16), preferred_element_type=F32
    ).astype(I32)
    running, count = running.astype(I32), count.astype(I32)
    first_window, shift = before >> 6, before & 63
    windows = [flag(lane == first_window + n) for n in range(3)]
    place = shift + running - 1
    window_of, slot_a = place >> 6, place & 63
    slot_b = slot_a + 64
    lane_of = jnp.zeros((ROWS, LANES), I32)
    for half in (64, 32, 16, 8, 4, 2, 1):
        seen = take(running, lane_of + (half - 1))
        lane_of = jnp.where(seen <= lane, lane_of + half, lane_of)
    turned = (lane - shift) & 127
    lane_of = take(lane_of, turned)
    used = turned < count
    in_front, behind = used & (lane >= shift), used & (lane < shift)

    for halo in halos:
        halo.wait_recv()
    loads[8].wait()

    def smooth(level):
        centre, below, above = row(cpl, level, LANES), row(cpl, level), row(cpl, level, 2 * LANES)
        low = pltpu.roll(jnp.where(lane == LANES - 1, below, centre), 1, 1)
        high = pltpu.roll(jnp.where(lane == 0, above, centre), LANES - 1, 1)
        return (low + 2.0 * centre + high) * 0.25

    def eliminate(step, carried):
        k_here, offset, factor = carried
        for n in range(4):
            level = LEV - 1 - n - 4 * step
            k_below = smooth(level - 1)
            inverse = 1.0 / (1.0 + k_below + k_here - k_here * factor)
            offset = (row(col, level) + k_here * offset) * inverse
            factor = k_below * inverse
            es[level] = offset
            fs[level] = factor
            k_here = k_below
        return k_here, offset, factor

    zeros = jnp.zeros((ROWS, LANES), F32)
    k_second, offset_two, factor_two = lax.fori_loop(0, (LEV - 2) // 4, eliminate, (zeros, zeros, zeros))
    k_base = smooth(0)
    pivot_base = 1.0 + k_second - k_second * factor_two
    right_one = row(col, 1) + k_second * offset_two
    old_ground = row(col, 0)
    loads[9].wait()

    arrive_ab()
    both = jnp.concatenate([ab_recv[:, pl.ds(0, LANES)], ab_recv[:, pl.ds(LANES, LANES)]], axis=0)
    stacked = jnp.concatenate(windows, axis=0)
    picked = lax.dot_general(
        jnp.concatenate([stacked] * 3, axis=1), jnp.concatenate(three_parts(both), axis=1),
        (((1,), (1,)), ((), ())), preferred_element_type=F32,
    )
    pieces = [picked[n * ROWS : (n + 1) * ROWS] for n in range(3)]

    def unpack(slot):
        found = [take(piece, slot) for piece in pieces]
        return jnp.where(window_of == 0, found[0], jnp.where(window_of == 1, found[1], found[2]))

    column_a = jnp.where(is_land, unpack(slot_a), sea_s[...])
    column_b = jnp.where(is_land, unpack(slot_b), 1.0)

    flux = jnp.zeros((ROWS, LANES), F32)
    ground_a, one_b = old_ground + column_a, 1.0 + column_b
    for _ in range(ITERS):
        k_ground = k_base * (1.0 + 0.5 * jnp.tanh(flux))
        pivot_one = pivot_base + k_ground
        surface = (ground_a * pivot_one + k_ground * right_one) / (one_b * pivot_one + k_ground * pivot_base)
        flux = column_a - column_b * surface
    inverse = 1.0 / pivot_one
    offset_one, factor_one = right_one * inverse, k_ground * inverse

    ordered = take(surface, lane_of)
    packed = jnp.concatenate([jnp.where(in_front, ordered, 0.0), jnp.where(behind, ordered, 0.0)], axis=0).T
    targets = jnp.concatenate(
        [
            jnp.concatenate([windows[0], windows[2]], axis=0),
            jnp.concatenate([windows[1], jnp.zeros((ROWS, LANES), BF16)], axis=0),
        ],
        axis=1,
    )
    placed = jnp.dot(
        jnp.concatenate(three_parts(packed), axis=1), jnp.concatenate([targets] * 3, axis=0),
        preferred_element_type=F32,
    )
    back_send[...] = placed[:ROWS, :LANES] + placed[ROWS:, LANES:]

    start_back, arrive_back, leave_back = exchange(back_send, back_recv, back_send_sem, back_recv_sem, lon, lev)
    start_back()
    back_recv[pl.ds(lon, 1), :] = back_send[pl.ds(lon, 1), :]

    stores = []
    value = offset_one + factor_one * surface
    col[pl.ds(0, 1), :] = surface.reshape(1, COLS)
    col[pl.ds(1, 1), :] = value.reshape(1, COLS)
    for group in range(0, LEV, 8):
        count_here = min(8, LEV - group)
        for level in range(max(group, 2), group + count_here):
            value = es[level] + fs[level] * value
            col[pl.ds(level, 1), :] = value.reshape(1, COLS)
        part = pl.ds(group, count_here)
        store = pltpu.make_async_copy(col.at[part, :], out_h.at[part, :], out_sem.at[group // 8])
        store.start()
        stores.append(store)

    arrive_back()
    land_surface = back_recv[...]
    for tile in range(NT):
        tile_o[pl.ds(tile, 1), :] = (scaled[tile] + coeff_r[tile] * land_surface).reshape(1, COLS)
    store = pltpu.make_async_copy(tile_o, tile_h, out_sem.at[9])
    store.start()
    stores.append(store)
    for halo in halos:
        halo.wait_send()
    leave_ab()
    leave_back()
    for store in stores:
        store.wait()


def on_device(column_old, coupling, sea_temp, land_mask, *tiles):
    any_space = pl.BlockSpec(memory_space=pl.ANY)
    levels, tile_rows = pltpu.VMEM((LEV, COLS), F32), pltpu.VMEM((NT, COLS), F32)
    plane = pltpu.VMEM((ROWS, LANES), F32)
    return pl.pallas_call(
        kernel,
        out_shape=(jax.ShapeDtypeStruct((LEV, COLS), F32), jax.ShapeDtypeStruct((NT, COLS), F32)),
        in_specs=[any_space] * 10,
        out_specs=(any_space, any_space),
        scratch_shapes=[
            levels,
            pltpu.VMEM((LEV - 1, COLS + 2 * LANES), F32),
            pltpu.VMEM((LEV, ROWS, LANES), F32),
            pltpu.VMEM((LEV, ROWS, LANES), F32),
            plane,
            pltpu.VMEM((ROWS, LANES), I32),
            *[tile_rows] * 6,
            pltpu.VMEM((NT, ROWS, LANES), F32),
            pltpu.VMEM((NT, ROWS, LANES), F32),
            tile_rows,
            pltpu.VMEM((N_LON, 2 * LANES), F32),
            pltpu.VMEM((N_LON, 2 * LANES), F32),
            plane,
            plane,
            pltpu.SemaphoreType.DMA((10,)),
            pltpu.SemaphoreType.DMA((2,)),
            pltpu.SemaphoreType.DMA((2,)),
            *[pltpu.SemaphoreType.DMA((N_LON - 1,))] * 4,
            pltpu.SemaphoreType.DMA((10,)),
        ],
        compiler_params=pltpu.CompilerParams(collective_id=0, has_side_effects=True),
    )(column_old, coupling, sea_temp.reshape(ROWS, LANES), land_mask.reshape(ROWS, LANES), *tiles)


def solution(mesh):
    columns, lines = P(None, ("lon", "lev")), P(("lon", "lev"))
    return jax.shard_map(
        on_device,
        mesh=mesh,
        in_specs=(columns, columns, lines, lines) + (columns,) * 6,
        out_specs=(columns, columns),
        check_vma=False,
    )
```

time: 218 us -> 39.7 us (0.18); the launches traced: 214 us -> 39.6 us
  local copies, waits for them, and re-layouts: 118 us -> 4.08 us
  Pallas kernels: 0 us -> 34.9 us
  other arithmetic: 34.1 us -> 0 us
  starting transfers between devices: 30.7 us -> 0 us
  waiting for transfers between devices: 16.7 us -> 0 us
  matrix products: 11.9 us -> 0 us
    slice x76 -> x0, local copies, waits for them, and re-layouts: 98.9 us -> none  [the longest x51 65.4 us: eliminate_upper(): lax.scan(eliminate_one_level, initial, (column_old[2:], k_below, k_above)...]
    pallas_call x0 -> x1, Pallas kernels: none -> 34.9 us  [on_device(): pl.pallas_call(kernel, out_shape=(jax.ShapeDtypeStruct((LEV, COLS), F32),...]
    all_to_all x3 -> x0, starting transfers between devices: 26.8 us -> none  [the longest x1 11.8 us: on_device(): lax.all_to_all(land_a.reshape(columns, 1), 'lon', split_axis=0, concat_ax...]
    dynamic_update_slice x34 -> x0, other arithmetic: 18.8 us -> none  [eliminate_upper(): lax.scan(eliminate_one_level, initial, (column_old[2:], k_below, k_above)...]
    all_to_all x3 -> x0, waiting for transfers between devices: 16.7 us -> none  [the longest x1 9.06 us: on_device(): lax.all_to_all(land_b.reshape(columns, 1), 'lon', split_axis=0, concat_ax...]
    dot_general x8 -> x0, matrix products: 11.9 us -> none  [the longest x1 5.83 us: unpack_rows(): jnp.einsum('mto,tio->mti', windows, selector, precision=HIGH, preferred_e...]
    reshape x4 -> x0, local copies, waits for them, and re-layouts: 11.4 us -> none  [the longest x3 8.82 us: eliminate_upper(): lax.scan(eliminate_one_level, initial, (column_old[2:], k_below, k_above)...]
    div x36 -> x0, other arithmetic: 4.64 us -> none  [the longest x1 2.29 us: on_device(): tile_temp = (source + tile_coeff * land_surface) / denominator]
  transfers between devices with their start and end apart: 5 -> 0, of which waited for: 2 -> 0; matrix products, arithmetic and copies ran while one was open for 53% -> 0% of each run, Pallas kernels for 0% -> 0%
where the time goes in v1:
time: 39.7 us; the launch traced here: 39.6 us
  Pallas kernels  34.9 us (88%)
  local copies, waits for them, and re-layouts  4.08 us (10%)
  between operations  0.65 us (2%)
    pallas_call x1, Pallas kernels, on_device(): pl.pallas_call(kernel, out_shape=(jax.ShapeDtypeStruct((LEV, COLS), F32),...  34.9 us
    unnamed x4, local copies, waits for them, and re-layouts  4.08 us

profile of v1, /device:TPU:1, one launch (start us, length us, event | category | flops | bytes accessed | tf_op | source)
XLA Modules:
  0.0 39.6 jit_solution(12685356230463289151)
XLA Ops:
  0.6 34.9 %shard_map.113 = (f32[70,8192]{1,0:T(8,128)}, f32[9,8192]{1,0:T(8,128)}) custom-call(f32[70,8192]{1,0:T(8,128)} %col_h.1, f32[69,8192]{1,0:T(8,128)} %cpl_h.1, f32[64,128]{1,0:T(8,128)} %bitcast.2, s32[64,128]{1,0:T(8,128)} %bitcast.3, f32[9,8192]{1,0:T(8,128)} %w_h.1, f32[9,8192]{1,0:T(8,128)} %co_h.1, f32[9,8192]{1,0:T(8,128)} %ca_h.1, f32[9,8192]{1,0:T(8,128)} %cd_h.1, ...), custom_call_target="tpu_custom_call" | custom-call | tf_op jit(solution)/shard_map/pallas_call | solution.py:284
  35.5 0.0 copy-start
  35.5 3.3 %copy.14 = f32[70,8192]{1,0:T(8,128)} copy(f32[70,8192]{1,0:T(8,128)} %get-tuple-element.4) | data formatting | bytes 4587520
  38.8 0.0 copy-done
  38.8 0.8 %copy.15 = f32[9,8192]{1,0:T(8,128)} copy(f32[9,8192]{1,0:T(8,128)S(1)} %copy-done) | data formatting | bytes 589824
Async XLA Ops:
  35.5 3.3 %copy-start = (f32[9,8192]{1,0:T(8,128)S(1)}, f32[9,8192]{1,0:T(8,128)}, u32[]{:S(2)}) copy-start(f32[9,8192]{1,0:T(8,128)} %get-tuple-element.5) | copy-start | bytes 884740

commit v2 on v1

v2 whole, which is shorter than its diff:
```python
import jax
import jax.numpy as jnp
from jax import lax
from jax.experimental import pallas as pl
from jax.experimental.pallas import tpu as pltpu
from jax.sharding import PartitionSpec as P

LEV = 70
NT = 9
COLS = 8192
ROWS = 64
LANES = 128
ITERS = 8
N_LON = 64
N_LEV = 4
N_Y = 4
N_Z = 8
MESH = pl.DeviceIdType.MESH
F32 = jnp.float32
BF16 = jnp.bfloat16
I32 = jnp.int32


def row(ref, level, start=0):
    return ref[pl.ds(level, 1), pl.ds(start, COLS)].reshape(ROWS, LANES)


def two_parts(value):
    high = value.astype(BF16)
    return jnp.concatenate([high, (value - high.astype(F32)).astype(BF16)], axis=1)


def take(value, index):
    return jnp.take_along_axis(value, index, axis=1, mode="promise_in_bounds")


def flag(condition):
    return jnp.where(condition, 1.0, 0.0).astype(BF16)


def iota(shape, dim):
    return lax.broadcasted_iota(I32, shape, dim)


def away(step, length):
    return min(step, length - step)


OFFSETS = sorted(
    [(dy, dz, other) for dy in range(N_Y) for dz in range(N_Z) for other in range(2) if dy + dz + other],
    key=lambda step: -(2 * away(step[0], N_Y) + 2 * away(step[1], N_Z) + step[2]),
)


def neighbours(lon):
    y, z, core = lon // (2 * N_Z), (lon // 2) % N_Z, lon % 2
    at_y = [(y + step) % N_Y * (2 * N_Z) for step in range(N_Y)]
    at_z = [(z + step) % N_Z * 2 for step in range(N_Z)]
    at_core = [core, 1 - core]
    to = [at_y[dy] + at_z[dz] + at_core[other] for dy, dz, other in OFFSETS]
    back = [at_y[-dy % N_Y] + at_z[-dz % N_Z] + at_core[other] for dy, dz, other in OFFSETS]
    return to, back


def exchange(send, recv, send_sem, recv_sem, peers, lon, lev):
    def copy(step, landing):
        return pltpu.make_async_remote_copy(
            src_ref=send.at[pl.ds(peers[0][step], 1), :], dst_ref=recv.at[pl.ds(landing, 1), :],
            send_sem=send_sem.at[step], recv_sem=recv_sem.at[step],
            device_id={"lon": peers[0][step], "lev": lev}, device_id_type=MESH,
        )

    steps = range(N_LON - 1)
    return [copy(step, lon) for step in steps], [copy(step, peers[1][step]) for step in steps]


def solve(k_base, pivot_base, right_one, old_ground, column_a, column_b):
    flux = jnp.zeros_like(k_base)
    ground_a, one_b = old_ground + column_a, 1.0 + column_b
    for _ in range(ITERS):
        k_ground = k_base * (1.0 + 0.5 * jnp.tanh(flux))
        pivot_one = pivot_base + k_ground
        surface = (ground_a * pivot_one + k_ground * right_one) / (one_b * pivot_one + k_ground * pivot_base)
        flux = column_a - column_b * surface
    return surface, k_ground, pivot_one


def kernel(
    col_h, cpl_h, sea_h, mask_h, w_h, co_h, ca_h, cd_h, old_h, fo_h,
    out, land_out, scaled, coeff_r,
    col, cpl, ks, es, fs, sea_s, mask_s, w_s, co_s, ca_s, cd_s, old_s, fo_s,
    ab_send, ab_recv, to_land, from_columns,
    in_sem, halo_send_sem, halo_recv_sem, ab_send_sem, ab_recv_sem, land_send_sem, land_recv_sem,
):
    lon, lev = lax.axis_index("lon"), lax.axis_index("lev")
    block = lon * N_LEV + lev
    right, left = (block + 1) % (N_LON * N_LEV), (block + N_LON * N_LEV - 1) % (N_LON * N_LEV)
    right_id = {"lon": right // N_LEV, "lev": right % N_LEV}
    left_id = {"lon": left // N_LEV, "lev": left % N_LEV}

    own = cpl.at[:, pl.ds(LANES, COLS)]
    pairs = [
        (mask_h, mask_s), (w_h, w_s), (co_h, co_s), (ca_h, ca_s), (cd_h, cd_s), (old_h, old_s), (fo_h, fo_s),
        (cpl_h, own), (col_h, col), (sea_h, sea_s),
    ]
    loads = [pltpu.make_async_copy(src, dst, in_sem.at[n]) for n, (src, dst) in enumerate(pairs)]
    for load in loads:
        load.start()

    barrier = pltpu.get_barrier_semaphore()

    peers = neighbours(lon)
    for peer in peers[0]:
        pl.semaphore_signal(barrier, inc=1, device_id={"lon": peer, "lev": lev}, device_id_type=MESH)
    for one in (left_id, right_id):
        pl.semaphore_signal(barrier, inc=1, device_id=one, device_id_type=MESH)

    for load in loads[:7]:
        load.wait()

    weight_sum = sum_a = sum_b = None
    for tile in range(NT):
        weight, coeff = row(w_s, tile), row(co_s, tile)
        capacity, conduct = row(ca_s, tile), row(cd_s, tile)
        held = capacity + conduct
        inverse = 1.0 / (capacity + coeff + conduct)
        source = capacity * row(old_s, tile) + row(fo_s, tile)
        ratio = coeff * inverse
        scaled[tile] = source * inverse
        coeff_r[tile] = ratio
        share = weight * ratio
        weight_sum = weight if tile == 0 else weight_sum + weight
        sum_a = share * source if tile == 0 else sum_a + share * source
        sum_b = share * held if tile == 0 else sum_b + share * held
    whole = 1.0 / weight_sum
    ab_send[:, pl.ds(0, LANES)] = sum_a * whole
    ab_send[:, pl.ds(LANES, LANES)] = sum_b * whole
    lane = iota((ROWS, LANES), 1)
    is_land = mask_s[...] == 1
    land = flag(is_land)
    running = jnp.dot(land, flag(iota((LANES, LANES), 0) <= iota((LANES, LANES), 1)), preferred_element_type=F32)
    count = jnp.dot(land, jnp.ones((LANES, LANES), BF16), preferred_element_type=F32)
    before = jnp.dot(
        flag(iota((ROWS, ROWS), 1) < iota((ROWS, ROWS), 0)), count.astype(BF16), preferred_element_type=F32
    ).astype(I32)
    running, count = running.astype(I32), count.astype(I32)
    first_window, shift = before >> 6, before & 63
    windows = [flag(lane == first_window + n) for n in range(3)]
    place = shift + running - 1
    window_of, slot_a = place >> 6, place & 63
    slot_b = slot_a + 64
    lane_of = jnp.zeros((ROWS, LANES), I32)
    for half in (64, 32, 16, 8, 4, 2, 1):
        seen = take(running, lane_of + (half - 1))
        lane_of = jnp.where(seen <= lane, lane_of + half, lane_of)
    turned = (lane - shift) & 127
    lane_of = take(lane_of, turned)
    used = turned < count
    in_front, behind = used & (lane >= shift), used & (lane < shift)

    loads[7].wait()
    pl.semaphore_wait(barrier, N_LON + 1)

    halos = [
        pltpu.make_async_remote_copy(
            src_ref=cpl.at[:, pl.ds(COLS, LANES)], dst_ref=cpl.at[:, pl.ds(0, LANES)],
            send_sem=halo_send_sem.at[0], recv_sem=halo_recv_sem.at[0], device_id=right_id, device_id_type=MESH,
        ),
        pltpu.make_async_remote_copy(
            src_ref=cpl.at[:, pl.ds(LANES, LANES)], dst_ref=cpl.at[:, pl.ds(COLS + LANES, LANES)],
            send_sem=halo_send_sem.at[1], recv_sem=halo_recv_sem.at[1], device_id=left_id, device_id_type=MESH,
        ),
    ]
    ab_out, ab_in = exchange(ab_send, ab_recv, ab_send_sem, ab_recv_sem, peers, lon, lev)
    for copy in halos + ab_out:
        copy.start()
    ab_recv[pl.ds(lon, 1), :] = ab_send[pl.ds(lon, 1), :]

    lane_wide = iota((LEV - 1, LANES), 1)

    def smooth(chunk):
        below, centre, above = (cpl[:, pl.ds((chunk + n) * LANES, LANES)] for n in range(3))
        low = pltpu.roll(jnp.where(lane_wide == LANES - 1, below, centre), 1, 1)
        high = pltpu.roll(jnp.where(lane_wide == 0, above, centre), LANES - 1, 1)
        ks[:, pl.ds(chunk * LANES, LANES)] = (low + 2.0 * centre + high) * 0.25

    for chunk in range(1, ROWS - 1):
        smooth(chunk)
    def eliminate(first, carried, k_row, old_row, keep):
        k_here, offset, top, bottom = carried
        for n in range(4):
            level = first - n
            k_below = k_row(level - 1)
            part = k_below * bottom
            pivot = part + top
            inverse = 1.0 / pivot
            offset = (old_row(level) + k_here * offset) * (bottom * inverse)
            factor = part * inverse
            keep(level, offset, factor)
            k_here, top, bottom = k_below, pivot + k_below * top, pivot
        return (k_here, offset, top * inverse, jnp.ones_like(top)), factor

    def start_of(shape):
        zeros, ones = jnp.zeros(shape, F32), jnp.ones(shape, F32)
        return (zeros, zeros, ones, ones), zeros

    def keep_all(level, offset, factor):
        es[level] = offset
        fs[level] = factor

    def all_columns(step, carried):
        return eliminate(
            LEV - 1 - 4 * step, carried[0], lambda level: row(ks, level), lambda level: row(col, level), keep_all
        )

    ks[:, pl.ds(0, LANES)] = jnp.ones((LEV - 1, LANES), F32)
    ks[:, pl.ds(COLS - LANES, LANES)] = jnp.ones((LEV - 1, LANES), F32)
    loads[8].wait()
    inner, inner_factor = lax.fori_loop(0, (LEV - 2) // 4, all_columns, start_of((ROWS, LANES)))

    for halo in halos:
        halo.wait_recv()
    smooth(0)
    smooth(ROWS - 1)
    sublane = iota((8, LANES), 0)

    def edge_row(ref, level):
        low, high = (ref[pl.ds(level, 1), pl.ds(start, 8 * LANES)].reshape(8, LANES) for start in (0, COLS - 8 * LANES))
        return jnp.where(sublane == 0, low, high)

    def keep_edges(level, offset, factor):
        for ref, value in ((es, offset), (fs, factor)):
            ref[level, pl.ds(0, 1), :] = value[0:1]
            ref[level, pl.ds(ROWS - 1, 1), :] = value[7:8]

    def edge_columns(step, carried):
        return eliminate(
            LEV - 1 - 4 * step, carried[0], lambda level: edge_row(ks, level), lambda level: edge_row(col, level), keep_edges
        )

    edge, edge_factor = lax.fori_loop(0, (LEV - 2) // 4, edge_columns, start_of((8, LANES)))

    def joined(all_rows, edges):
        first = jnp.where(sublane == 0, edges, all_rows[0:8])
        last = jnp.where(sublane == 7, edges, all_rows[ROWS - 8 :])
        return jnp.concatenate([first, all_rows[8 : ROWS - 8], last], axis=0)

    k_second, offset_two, pivot_base = (joined(inner[n], edge[n]) for n in range(3))
    k_base = row(ks, 0)
    right_one = row(col, 1) + k_second * offset_two
    old_ground = row(col, 0)

    targets = jnp.concatenate(
        [
            jnp.concatenate([windows[0], windows[2]], axis=0),
            jnp.concatenate([windows[1], jnp.zeros((ROWS, LANES), BF16)], axis=0),
        ],
        axis=1,
    )
    fields = (k_base, pivot_base, right_one, old_ground)
    turned_fields = []
    for field in fields:
        ordered = take(field, lane_of)
        turned_fields.append(
            jnp.concatenate([jnp.where(in_front, ordered, 0.0), jnp.where(behind, ordered, 0.0)], axis=0).T
        )
    placed = jnp.dot(
        two_parts(jnp.concatenate(turned_fields, axis=0)), jnp.concatenate([targets] * 2, axis=0),
        preferred_element_type=F32,
    )
    for n in range(len(fields)):
        top = 2 * ROWS * n
        to_land[:, pl.ds(n * LANES, LANES)] = (
            placed[top : top + ROWS, :LANES] + placed[top + ROWS : top + 2 * ROWS, LANES:]
        )
    land_outgoing, land_incoming = exchange(to_land, from_columns, land_send_sem, land_recv_sem, peers, lon, lev)
    for copy in land_outgoing:
        copy.start()
    from_columns[pl.ds(lon, 1), :] = to_land[pl.ds(lon, 1), :]
    loads[9].wait()

    for copy in ab_in:
        copy.wait_recv()
    both = jnp.concatenate([ab_recv[:, pl.ds(0, LANES)], ab_recv[:, pl.ds(LANES, LANES)]], axis=0)
    stacked = jnp.concatenate(windows, axis=0)
    picked = lax.dot_general(
        jnp.concatenate([stacked] * 2, axis=1), two_parts(both),
        (((1,), (1,)), ((), ())), preferred_element_type=F32,
    )
    pieces = [picked[n * ROWS : (n + 1) * ROWS] for n in range(3)]

    def unpack(slot):
        found = [take(piece, slot) for piece in pieces]
        return jnp.where(window_of == 0, found[0], jnp.where(window_of == 1, found[1], found[2]))

    column_a = jnp.where(is_land, unpack(slot_a), sea_s[...])
    column_b = jnp.where(is_land, unpack(slot_b), 1.0)

    surface, k_ground, pivot_one = solve(*fields, column_a, column_b)
    inverse = 1.0 / pivot_one
    offset_one, factor_one = right_one * inverse, k_ground * inverse

    value = offset_one + factor_one * surface
    out[pl.ds(0, 1), :] = surface.reshape(1, COLS)
    out[pl.ds(1, 1), :] = value.reshape(1, COLS)
    for level in range(2, LEV):
        value = es[level] + fs[level] * value
        out[pl.ds(level, 1), :] = value.reshape(1, COLS)

    for copy in halos + ab_out + land_outgoing:
        copy.wait_send()
    for copy in land_incoming:
        copy.wait_recv()
    land_out[:, pl.ds(0, 4 * LANES)] = from_columns[...]
    land_out[:, pl.ds(4 * LANES, 2 * LANES)] = ab_send[...]


def finish(out, land, scaled, coeff_r, out_h, tile_h, tile_o, sems):
    stores = []
    for first in range(0, LEV, 8):
        part = pl.ds(first, min(8, LEV - first))
        stores.append(pltpu.make_async_copy(out.at[part, :], out_h.at[part, :], sems.at[1 + first // 8]))
        stores[-1].start()
    k_base, pivot_base, right_one, old_ground, land_a, land_b = (land[:, pl.ds(n * LANES, LANES)] for n in range(6))
    taken = pivot_base > 0.0
    surface, _, _ = solve(k_base, jnp.where(taken, pivot_base, 1.0), right_one, old_ground, land_a, land_b)
    land_surface = jnp.where(taken, surface, 0.0)
    for tile in range(NT):
        tile_o[pl.ds(tile, 1), :] = (scaled[tile] + coeff_r[tile] * land_surface).reshape(1, COLS)
    stores.append(pltpu.make_async_copy(tile_o, tile_h, sems.at[0]))
    stores[-1].start()
    for store in stores:
        store.wait()


def on_device(column_old, coupling, sea_temp, land_mask, *tiles):
    any_space = pl.BlockSpec(memory_space=pl.ANY)
    levels, tile_rows = pltpu.VMEM((LEV, COLS), F32), pltpu.VMEM((NT, COLS), F32)
    plane = pltpu.VMEM((ROWS, LANES), F32)
    in_vmem = pl.BlockSpec(memory_space=pltpu.VMEM)
    arrays = (column_old, coupling, sea_temp.reshape(ROWS, LANES), land_mask.reshape(ROWS, LANES), *tiles)
    tile_planes = pltpu.VMEM((NT, ROWS, LANES), F32)
    results = pl.pallas_call(
        kernel,
        out_shape=(levels, pltpu.VMEM((ROWS, 6 * LANES), F32), tile_planes, tile_planes),
        in_specs=[any_space] * 10,
        out_specs=(in_vmem,) * 4,
        scratch_shapes=[
            levels,
            pltpu.VMEM((LEV - 1, COLS + 2 * LANES), F32),
            pltpu.VMEM((LEV - 1, COLS), F32),
            pltpu.VMEM((LEV, ROWS, LANES), F32),
            pltpu.VMEM((LEV, ROWS, LANES), F32),
            plane,
            pltpu.VMEM((ROWS, LANES), I32),
            *[tile_rows] * 6,
            *[pltpu.VMEM((N_LON, 2 * LANES), F32)] * 2,
            *[pltpu.VMEM((N_LON, 4 * LANES), F32)] * 2,
            pltpu.SemaphoreType.DMA((10,)),
            pltpu.SemaphoreType.DMA((2,)),
            pltpu.SemaphoreType.DMA((2,)),
            *[pltpu.SemaphoreType.DMA((N_LON - 1,))] * 4,
        ],
        compiler_params=pltpu.CompilerParams(
            collective_id=0, has_side_effects=True, vmem_limit_bytes=24 * 2**20
        ),
    )(*[pltpu.with_memory_space_constraint(array, pltpu.HBM) for array in arrays])
    return pl.pallas_call(
        finish,
        out_shape=(jax.ShapeDtypeStruct((LEV, COLS), F32), jax.ShapeDtypeStruct((NT, COLS), F32)),
        in_specs=[in_vmem] * 4,
        out_specs=(any_space, any_space),
        scratch_shapes=[tile_rows, pltpu.SemaphoreType.DMA((10,))],
        compiler_params=pltpu.CompilerParams(vmem_limit_bytes=4 * 2**20),
    )(*results)


def solution(mesh):
    columns, lines = P(None, ("lon", "lev")), P(("lon", "lev"))
    return jax.shard_map(
        on_device,
        mesh=mesh,
        in_specs=(columns, columns, lines, lines) + (columns,) * 6,
        out_specs=(columns, columns),
        check_vma=False,
    )
```

time: 39.7 us -> 27.3 us (0.69)
  Pallas kernels: 34.9 us -> 26.6 us
  local copies, waits for them, and re-layouts: 4.08 us -> 0 us
    pallas_call x1 -> x2, Pallas kernels: 34.9 us -> 26.6 us  [the longest x1 25 us: on_device(): pl.pallas_call(kernel, out_shape=(levels, pltpu.VMEM((ROWS, 6 * LANES), F...]
    unnamed x4 -> x0, local copies, waits for them, and re-layouts: 4.08 us -> none
where the time goes in v2:
time: 27.3 us
  Pallas kernels  26.6 us (97%)
  between operations  0.64 us (2%)
    pallas_call x1, Pallas kernels, on_device(): pl.pallas_call(kernel, out_shape=(levels, pltpu.VMEM((ROWS, 6 * LANES), F...  25 us
    pallas_call x1, Pallas kernels, on_device(): pl.pallas_call(finish, out_shape=(jax.ShapeDtypeStruct((LEV, COLS), F32),...  1.66 us

profile of v2, /device:TPU:1, one launch (start us, length us, event | category | flops | bytes accessed | tf_op | source)
XLA Modules:
  0.0 27.3 jit_solution(12503753073598526781)
XLA Ops:
  0.6 25.0 %shard_map.113 = (f32[70,8192]{1,0:T(8,128)S(1)}, f32[64,768]{1,0:T(8,128)S(1)}, f32[9,64,128]{2,1,0:T(8,128)S(1)}, f32[9,64,128]{2,1,0:T(8,128)S(1)}) custom-call(f32[70,8192]{1,0:T(8,128)} %col_h.1, f32[69,8192]{1,0:T(8,128)} %cpl_h.1, f32[64,128]{1,0:T(8,128)} %bitcast.2, s32[64,128]{1,0:T(8,128)} %bitcast.3, f32[9,8192]{1,0:T(8,128)} %w_h.1, ...), custom_call_target="tpu_custom_call" | custom-call | tf_op jit(solution)/shard_map/pallas_call | solution.py:343
  25.6 1.7 %shard_map.114 = (f32[70,8192]{1,0:T(8,128)}, f32[9,8192]{1,0:T(8,128)}) custom-call(f32[70,8192]{1,0:T(8,128)S(1)} %get-tuple-element.6.out, f32[64,768]{1,0:T(8,128)S(1)} %get-tuple-element.7.land, f32[9,64,128]{2,1,0:T(8,128)S(1)} %get-tuple-element.8.scaled, f32[9,64,128]{2,1,0:T(8,128)S(1)} %get-tuple-element.9.coeff_r), custom_call_target="tpu_custom_call" | custom-call | tf_op jit(solution)/shard_map/pallas_call | solution.py:368

commit v3 on v2

--- a/solution.py
+++ b/solution.py
@@ -57,21 +57,21 @@
     at_y = [(y + step) % N_Y * (2 * N_Z) for step in range(N_Y)]
     at_z = [(z + step) % N_Z * 2 for step in range(N_Z)]
     at_core = [core, 1 - core]
-    to = [at_y[dy] + at_z[dz] + at_core[other] for dy, dz, other in OFFSETS]
-    back = [at_y[-dy % N_Y] + at_z[-dz % N_Z] + at_core[other] for dy, dz, other in OFFSETS]
-    return to, back
-
-
-def exchange(send, recv, send_sem, recv_sem, peers, lon, lev):
-    def copy(step, landing):
-        return pltpu.make_async_remote_copy(
-            src_ref=send.at[pl.ds(peers[0][step], 1), :], dst_ref=recv.at[pl.ds(landing, 1), :],
-            send_sem=send_sem.at[step], recv_sem=recv_sem.at[step],
-            device_id={"lon": peers[0][step], "lev": lev}, device_id_type=MESH,
-        )
-
-    steps = range(N_LON - 1)
-    return [copy(step, lon) for step in steps], [copy(step, peers[1][step]) for step in steps]
+    return [at_y[dy] + at_z[dz] + at_core[other] for dy, dz, other in OFFSETS]
+
+
+def exchange(send, recv, total, sems, peers, lon, lev):
+    copies = [
+        pltpu.make_async_remote_copy(
+            src_ref=send.at[pl.ds(peer, 1), :], dst_ref=recv.at[pl.ds(lon, 1), :], send_sem=sems.at[0], recv_sem=sems.at[1],
+            device_id={"lon": peer, "lev": lev}, device_id_type=MESH,
+        )
+        for peer in peers
+    ]
+    return copies, pltpu.make_async_remote_copy(
+        src_ref=total, dst_ref=total, send_sem=sems.at[0], recv_sem=sems.at[1],
+        device_id={"lon": peers[0], "lev": lev}, device_id_type=MESH,
+    )
 
 
 def solve(k_base, pivot_base, right_one, old_ground, column_a, column_b):
@@ -90,7 +90,7 @@
     out, land_out, scaled, coeff_r,
     col, cpl, ks, es, fs, sea_s, mask_s, w_s, co_s, ca_s, cd_s, old_s, fo_s,
     ab_send, ab_recv, to_land, from_columns,
-    in_sem, halo_send_sem, halo_recv_sem, ab_send_sem, ab_recv_sem, land_send_sem, land_recv_sem,
+    ab_total, land_total, in_sem, halo_send_sem, halo_recv_sem, ab_sems, land_sems,
 ):
     lon, lev = lax.axis_index("lon"), lax.axis_index("lev")
     block = lon * N_LEV + lev
@@ -100,8 +100,8 @@
 
     own = cpl.at[:, pl.ds(LANES, COLS)]
     pairs = [
-        (mask_h, mask_s), (w_h, w_s), (co_h, co_s), (ca_h, ca_s), (cd_h, cd_s), (old_h, old_s), (fo_h, fo_s),
-        (cpl_h, own), (col_h, col), (sea_h, sea_s),
+        (co_h, co_s), (ca_h, ca_s), (cd_h, cd_s), (old_h, old_s), (fo_h, fo_s), (w_h, w_s), (cpl_h, own), (mask_h, mask_s),
+        (col_h, col), (sea_h, sea_s),
     ]
     loads = [pltpu.make_async_copy(src, dst, in_sem.at[n]) for n, (src, dst) in enumerate(pairs)]
     for load in loads:
@@ -109,13 +109,13 @@
 
     barrier = pltpu.get_barrier_semaphore()
 
-    peers = neighbours(lon)
-    for peer in peers[0]:
-        pl.semaphore_signal(barrier, inc=1, device_id={"lon": peer, "lev": lev}, device_id_type=MESH)
     for one in (left_id, right_id):
         pl.semaphore_signal(barrier, inc=1, device_id=one, device_id_type=MESH)
-
-    for load in loads[:7]:
+    peers = neighbours(lon)
+    for peer in peers:
+        pl.semaphore_signal(barrier, inc=1, device_id={"lon": peer, "lev": lev}, device_id_type=MESH)
+
+    for load in loads[:6]:
         load.wait()
 
     weight_sum = sum_a = sum_b = None
@@ -135,7 +135,28 @@
     whole = 1.0 / weight_sum
     ab_send[:, pl.ds(0, LANES)] = sum_a * whole
     ab_send[:, pl.ds(LANES, LANES)] = sum_b * whole
+    loads[6].wait()
+    pl.semaphore_wait(barrier, N_LON + 1)
+
+    halos = [
+        pltpu.make_async_remote_copy(
+            src_ref=cpl.at[:, pl.ds(COLS, LANES)], dst_ref=cpl.at[:, pl.ds(0, LANES)],
+            send_sem=halo_send_sem.at[0], recv_sem=halo_recv_sem.at[0], device_id=right_id, device_id_type=MESH,
+        ),
+        pltpu.make_async_remote_copy(
+            src_ref=cpl.at[:, pl.ds(LANES, LANES)], dst_ref=cpl.at[:, pl.ds(COLS + LANES, LANES)],
+            send_sem=halo_send_sem.at[1], recv_sem=halo_recv_sem.at[1], device_id=left_id, device_id_type=MESH,
+        ),
+    ]
+    for halo in halos:
+        halo.start()
+    ab_out, ab_all = exchange(ab_send, ab_recv, ab_total, ab_sems, peers, lon, lev)
+    for copy in ab_out:
+        copy.start()
+    ab_recv[pl.ds(lon, 1), :] = ab_send[pl.ds(lon, 1), :]
+
     lane = iota((ROWS, LANES), 1)
+    loads[7].wait()
     is_land = mask_s[...] == 1
     land = flag(is_land)
     running = jnp.dot(land, flag(iota((LANES, LANES), 0) <= iota((LANES, LANES), 1)), preferred_element_type=F32)
@@ -158,24 +179,6 @@
     used = turned < count
     in_front, behind = used & (lane >= shift), used & (lane < shift)
 
-    loads[7].wait()
-    pl.semaphore_wait(barrier, N_LON + 1)
-
-    halos = [
-        pltpu.make_async_remote_copy(
-            src_ref=cpl.at[:, pl.ds(COLS, LANES)], dst_ref=cpl.at[:, pl.ds(0, LANES)],
-            send_sem=halo_send_sem.at[0], recv_sem=halo_recv_sem.at[0], device_id=right_id, device_id_type=MESH,
-        ),
-        pltpu.make_async_remote_copy(
-            src_ref=cpl.at[:, pl.ds(LANES, LANES)], dst_ref=cpl.at[:, pl.ds(COLS + LANES, LANES)],
-            send_sem=halo_send_sem.at[1], recv_sem=halo_recv_sem.at[1], device_id=left_id, device_id_type=MESH,
-        ),
-    ]
-    ab_out, ab_in = exchange(ab_send, ab_recv, ab_send_sem, ab_recv_sem, peers, lon, lev)
-    for copy in halos + ab_out:
-        copy.start()
-    ab_recv[pl.ds(lon, 1), :] = ab_send[pl.ds(lon, 1), :]
-
     lane_wide = iota((LEV - 1, LANES), 1)
 
     def smooth(chunk):
@@ -273,14 +276,13 @@
         to_land[:, pl.ds(n * LANES, LANES)] = (
             placed[top : top + ROWS, :LANES] + placed[top + ROWS : top + 2 * ROWS, LANES:]
         )
-    land_outgoing, land_incoming = exchange(to_land, from_columns, land_send_sem, land_recv_sem, peers, lon, lev)
+    land_outgoing, land_all = exchange(to_land, from_columns, land_total, land_sems, peers, lon, lev)
     for copy in land_outgoing:
         copy.start()
     from_columns[pl.ds(lon, 1), :] = to_land[pl.ds(lon, 1), :]
     loads[9].wait()
 
-    for copy in ab_in:
-        copy.wait_recv()
+    ab_all.wait_recv()
     both = jnp.concatenate([ab_recv[:, pl.ds(0, LANES)], ab_recv[:, pl.ds(LANES, LANES)]], axis=0)
     stacked = jnp.concatenate(windows, axis=0)
     picked = lax.dot_general(
@@ -307,10 +309,9 @@
         value = es[level] + fs[level] * value
         out[pl.ds(level, 1), :] = value.reshape(1, COLS)
 
-    for copy in halos + ab_out + land_outgoing:
+    for copy in (*halos, ab_all, land_all):
         copy.wait_send()
-    for copy in land_incoming:
-        copy.wait_recv()
+    land_all.wait_recv()
     land_out[:, pl.ds(0, 4 * LANES)] = from_columns[...]
     land_out[:, pl.ds(4 * LANES, 2 * LANES)] = ab_send[...]
 
@@ -356,10 +357,13 @@
             *[tile_rows] * 6,
             *[pltpu.VMEM((N_LON, 2 * LANES), F32)] * 2,
             *[pltpu.VMEM((N_LON, 4 * LANES), F32)] * 2,
+            pltpu.VMEM(((N_LON - 1) * 2, LANES), F32),
+            pltpu.VMEM(((N_LON - 1) * 4, LANES), F32),
             pltpu.SemaphoreType.DMA((10,)),
             pltpu.SemaphoreType.DMA((2,)),
             pltpu.SemaphoreType.DMA((2,)),
-            *[pltpu.SemaphoreType.DMA((N_LON - 1,))] * 4,
+            pltpu.SemaphoreType.DMA((2,)),
+            pltpu.SemaphoreType.DMA((2,)),
         ],
         compiler_params=pltpu.CompilerParams(
             collective_id=0, has_side_effects=True, vmem_limit_bytes=24 * 2**20

time: 27.3 us -> 25 us (0.916)
  Pallas kernels: 26.6 us -> 24.3 us
    pallas_call x1, Pallas kernels: 25 us -> 22.7 us  [on_device(): pl.pallas_call(kernel, out_shape=(levels, pltpu.VMEM((ROWS, 6 * LANES), F...]
where the time goes in v3:
time: 25 us
  Pallas kernels  24.3 us (97%)
  between operations  0.64 us (3%)
    pallas_call x1, Pallas kernels, on_device(): pl.pallas_call(kernel, out_shape=(levels, pltpu.VMEM((ROWS, 6 * LANES), F...  22.7 us
    pallas_call x1, Pallas kernels, on_device(): pl.pallas_call(finish, out_shape=(jax.ShapeDtypeStruct((LEV, COLS), F32),...  1.66 us

profile of v3, /device:TPU:1, one launch (start us, length us, event | category | flops | bytes accessed | tf_op | source)
XLA Modules:
  0.0 25.0 jit_solution(2974754960753187867)
XLA Ops:
  0.6 22.7 %shard_map.113 = (f32[70,8192]{1,0:T(8,128)S(1)}, f32[64,768]{1,0:T(8,128)S(1)}, f32[9,64,128]{2,1,0:T(8,128)S(1)}, f32[9,64,128]{2,1,0:T(8,128)S(1)}) custom-call(f32[70,8192]{1,0:T(8,128)} %col_h.1, f32[69,8192]{1,0:T(8,128)} %cpl_h.1, f32[64,128]{1,0:T(8,128)} %bitcast.2, s32[64,128]{1,0:T(8,128)} %bitcast.3, f32[9,8192]{1,0:T(8,128)} %w_h.1, ...), custom_call_target="tpu_custom_call" | custom-call | tf_op jit(solution)/shard_map/pallas_call | solution.py:344
  23.3 1.7 %shard_map.114 = (f32[70,8192]{1,0:T(8,128)}, f32[9,8192]{1,0:T(8,128)}) custom-call(f32[70,8192]{1,0:T(8,128)S(1)} %get-tuple-element.6.out, f32[64,768]{1,0:T(8,128)S(1)} %get-tuple-element.7.land, f32[9,64,128]{2,1,0:T(8,128)S(1)} %get-tuple-element.8.scaled, f32[9,64,128]{2,1,0:T(8,128)S(1)} %get-tuple-element.9.coeff_r), custom_call_target="tpu_custom_call" | custom-call | tf_op jit(solution)/shard_map/pallas_call | solution.py:372

commit v4 on v3

--- a/solution.py
+++ b/solution.py
@@ -178,80 +178,57 @@
     lane_of = take(lane_of, turned)
     used = turned < count
     in_front, behind = used & (lane >= shift), used & (lane < shift)
+    line = iota((ROWS, LANES), 0)
+    last = jnp.broadcast_to((before + count)[ROWS - 1 :, :], (ROWS, LANES)) - 1
+    last_flag = jnp.broadcast_to(mask_s[pl.ds(ROWS - 1, 1), :][:, LANES - 1 :], (ROWS, LANES))
+    first_column, last_column = (line == 0) & (lane == 0), (line == ROWS - 1) & (lane == LANES - 1)
+    first_slot = first_column & is_land
+    last_slot = (line == (last & 63)) & (lane == (last >> 6)) & (last_flag == 1)
 
     lane_wide = iota((LEV - 1, LANES), 1)
 
-    def smooth(chunk):
-        below, centre, above = (cpl[:, pl.ds((chunk + n) * LANES, LANES)] for n in range(3))
+    def smooth(chunk, under=0, over=2):
+        below, centre, above = (cpl[:, pl.ds((chunk + n) * LANES, LANES)] for n in (under, 1, over))
         low = pltpu.roll(jnp.where(lane_wide == LANES - 1, below, centre), 1, 1)
         high = pltpu.roll(jnp.where(lane_wide == 0, above, centre), LANES - 1, 1)
         ks[:, pl.ds(chunk * LANES, LANES)] = (low + 2.0 * centre + high) * 0.25
 
+    smooth(0, under=1)
+    smooth(ROWS - 1, over=1)
     for chunk in range(1, ROWS - 1):
         smooth(chunk)
-    def eliminate(first, carried, k_row, old_row, keep):
+    def eliminate(level, carried, k_row, old_row, keep):
         k_here, offset, top, bottom = carried
-        for n in range(4):
-            level = first - n
-            k_below = k_row(level - 1)
-            part = k_below * bottom
-            pivot = part + top
-            inverse = 1.0 / pivot
-            offset = (old_row(level) + k_here * offset) * (bottom * inverse)
-            factor = part * inverse
-            keep(level, offset, factor)
-            k_here, top, bottom = k_below, pivot + k_below * top, pivot
-        return (k_here, offset, top * inverse, jnp.ones_like(top)), factor
+        k_below = k_row(level - 1)
+        part = k_below * bottom
+        pivot = part + top
+        inverse = 1.0 / pivot
+        offset = (old_row(level) + k_here * offset) * (bottom * inverse)
+        keep(level, offset, part * inverse)
+        return (k_below, offset, part + (1.0 + k_below) * top, pivot), inverse
+
+    def scaled_down(carried, inverse):
+        k_here, offset, top, _ = carried
+        return k_here, offset, top * inverse, jnp.ones_like(top)
 
     def start_of(shape):
         zeros, ones = jnp.zeros(shape, F32), jnp.ones(shape, F32)
-        return (zeros, zeros, ones, ones), zeros
+        return zeros, zeros, ones, ones
 
     def keep_all(level, offset, factor):
         es[level] = offset
         fs[level] = factor
 
     def all_columns(step, carried):
-        return eliminate(
-            LEV - 1 - 4 * step, carried[0], lambda level: row(ks, level), lambda level: row(col, level), keep_all
-        )
-
-    ks[:, pl.ds(0, LANES)] = jnp.ones((LEV - 1, LANES), F32)
-    ks[:, pl.ds(COLS - LANES, LANES)] = jnp.ones((LEV - 1, LANES), F32)
+        for n in range(4):
+            carried, inverse = eliminate(
+                LEV - 1 - 4 * step - n, carried, lambda level: row(ks, level), lambda level: row(col, level), keep_all
+            )
+        return scaled_down(carried, inverse)
+
     loads[8].wait()
-    inner, inner_factor = lax.fori_loop(0, (LEV - 2) // 4, all_columns, start_of((ROWS, LANES)))
-
-    for halo in halos:
-        halo.wait_recv()
-    smooth(0)
-    smooth(ROWS - 1)
-    sublane = iota((8, LANES), 0)
-
-    def edge_row(ref, level):
-        low, high = (ref[pl.ds(level, 1), pl.ds(start, 8 * LANES)].reshape(8, LANES) for start in (0, COLS - 8 * LANES))
-        return jnp.where(sublane == 0, low, high)
-
-    def keep_edges(level, offset, factor):
-        for ref, value in ((es, offset), (fs, factor)):
-            ref[level, pl.ds(0, 1), :] = value[0:1]
-            ref[level, pl.ds(ROWS - 1, 1), :] = value[7:8]
-
-    def edge_columns(step, carried):
-        return eliminate(
-            LEV - 1 - 4 * step, carried[0], lambda level: edge_row(ks, level), lambda level: edge_row(col, level), keep_edges
-        )
-
-    edge, edge_factor = lax.fori_loop(0, (LEV - 2) // 4, edge_columns, start_of((8, LANES)))
-
-    def joined(all_rows, edges):
-        first = jnp.where(sublane == 0, edges, all_rows[0:8])
-        last = jnp.where(sublane == 7, edges, all_rows[ROWS - 8 :])
-        return jnp.concatenate([first, all_rows[8 : ROWS - 8], last], axis=0)
-
-    k_second, offset_two, pivot_base = (joined(inner[n], edge[n]) for n in range(3))
-    k_base = row(ks, 0)
-    right_one = row(col, 1) + k_second * offset_two
-    old_ground = row(col, 0)
+    k_second, offset_two, pivot_base, _ = lax.fori_loop(0, (LEV - 2) // 4, all_columns, start_of((ROWS, LANES)))
+    fields = [row(ks, 0), pivot_base, row(col, 1) + k_second * offset_two, row(col, 0)]
 
     targets = jnp.concatenate(
         [
@@ -260,10 +237,9 @@
         ],
         axis=1,
     )
-    fields = (k_base, pivot_base, right_one, old_ground)
     turned_fields = []
     for field in fields:
-        ordered = take(field, lane_of)
+        ordered = take(jnp.where(first_column | last_column, 0.0, field), lane_of)
         turned_fields.append(
             jnp.concatenate([jnp.where(in_front, ordered, 0.0), jnp.where(behind, ordered, 0.0)], axis=0).T
         )
@@ -276,11 +252,48 @@
         to_land[:, pl.ds(n * LANES, LANES)] = (
             placed[top : top + ROWS, :LANES] + placed[top + ROWS : top + 2 * ROWS, LANES:]
         )
+
+    for halo in halos:
+        halo.wait_recv()
+    smooth(0)
+    smooth(ROWS - 1)
+    sublane = iota((8, LANES), 0)
+
+    def edge_row(ref, level):
+        low, high = (ref[pl.ds(level, 1), pl.ds(start, 8 * LANES)].reshape(8, LANES) for start in (0, COLS - 8 * LANES))
+        return jnp.where(sublane == 0, low, high)
+
+    def keep_edges(level, offset, factor):
+        for ref, value in ((es, offset), (fs, factor)):
+            ref[level, pl.ds(0, 1), :] = value[0:1]
+            ref[level, pl.ds(ROWS - 1, 1), :] = value[7:8]
+
+    edge = start_of((8, LANES))
+    for level in range(LEV - 1, 1, -1):
+        edge, inverse = eliminate(
+            level, edge, lambda level: edge_row(ks, level), lambda level: edge_row(col, level), keep_edges
+        )
+        if level % 12 == 2:
+            edge = scaled_down(edge, inverse)
+    edge_fields = [edge_row(ks, 0), edge[2], edge_row(col, 1) + edge[0] * edge[1], edge_row(col, 0)]
+
+    for n, value in enumerate(edge_fields):
+        part = pl.ds(n * LANES, LANES)
+        first_value, last_value = value[0:1, 0:1], value[7:8, LANES - 1 :]
+        to_land[:, part] = jnp.where(first_slot, first_value, jnp.where(last_slot, last_value, to_land[:, part]))
     land_outgoing, land_all = exchange(to_land, from_columns, land_total, land_sems, peers, lon, lev)
     for copy in land_outgoing:
         copy.start()
     from_columns[pl.ds(lon, 1), :] = to_land[pl.ds(lon, 1), :]
     loads[9].wait()
+
+    def joined(all_rows, edges):
+        first = jnp.where(sublane == 0, edges, all_rows[0:8])
+        last_rows = jnp.where(sublane == 7, edges, all_rows[ROWS - 8 :])
+        return jnp.concatenate([first, all_rows[8 : ROWS - 8], last_rows], axis=0)
+
+    fields = [joined(field, edges) for field, edges in zip(fields, edge_fields)]
+    right_one = fields[2]
 
     ab_all.wait_recv()
     both = jnp.concatenate([ab_recv[:, pl.ds(0, LANES)], ab_recv[:, pl.ds(LANES, LANES)]], axis=0)
@@ -317,19 +330,15 @@
 
 
 def finish(out, land, scaled, coeff_r, out_h, tile_h, tile_o, sems):
-    stores = []
-    for first in range(0, LEV, 8):
-        part = pl.ds(first, min(8, LEV - first))
-        stores.append(pltpu.make_async_copy(out.at[part, :], out_h.at[part, :], sems.at[1 + first // 8]))
-        stores[-1].start()
+    stores = [pltpu.make_async_copy(out, out_h, sems.at[0]), pltpu.make_async_copy(tile_o, tile_h, sems.at[1])]
+    stores[0].start()
     k_base, pivot_base, right_one, old_ground, land_a, land_b = (land[:, pl.ds(n * LANES, LANES)] for n in range(6))
     taken = pivot_base > 0.0
     surface, _, _ = solve(k_base, jnp.where(taken, pivot_base, 1.0), right_one, old_ground, land_a, land_b)
     land_surface = jnp.where(taken, surface, 0.0)
     for tile in range(NT):
         tile_o[pl.ds(tile, 1), :] = (scaled[tile] + coeff_r[tile] * land_surface).reshape(1, COLS)
-    stores.append(pltpu.make_async_copy(tile_o, tile_h, sems.at[0]))
-    stores[-1].start()
+    stores[1].start()
     for store in stores:
         store.wait()
 
@@ -374,7 +383,7 @@
         out_shape=(jax.ShapeDtypeStruct((LEV, COLS), F32), jax.ShapeDtypeStruct((NT, COLS), F32)),
         in_specs=[in_vmem] * 4,
         out_specs=(any_space, any_space),
-        scratch_shapes=[tile_rows, pltpu.SemaphoreType.DMA((10,))],
+        scratch_shapes=[tile_rows, pltpu.SemaphoreType.DMA((2,))],
         compiler_params=pltpu.CompilerParams(vmem_limit_bytes=4 * 2**20),
     )(*results)
 

time: 25 us -> 24.4 us (0.976)
  Pallas kernels: 24.3 us -> 23.6 us
    pallas_call x1, Pallas kernels: 22.7 us -> 22 us  [on_device(): pl.pallas_call(kernel, out_shape=(levels, pltpu.VMEM((ROWS, 6 * LANES), F...]
where the time goes in v4:
time: 24.4 us; the launch traced here: 24.3 us
  Pallas kernels  23.6 us (97%)
  between operations  0.64 us (3%)
    pallas_call x1, Pallas kernels, on_device(): pl.pallas_call(kernel, out_shape=(levels, pltpu.VMEM((ROWS, 6 * LANES), F...  22 us
    pallas_call x1, Pallas kernels, on_device(): pl.pallas_call(finish, out_shape=(jax.ShapeDtypeStruct((LEV, COLS), F32),...  1.59 us

profile of v4, /device:TPU:1, one launch (start us, length us, event | category | flops | bytes accessed | tf_op | source)
XLA Modules:
  0.0 24.3 jit_solution(9105318771686388454)
XLA Ops:
  0.6 22.0 %shard_map.113 = (f32[70,8192]{1,0:T(8,128)S(1)}, f32[64,768]{1,0:T(8,128)S(1)}, f32[9,64,128]{2,1,0:T(8,128)S(1)}, f32[9,64,128]{2,1,0:T(8,128)S(1)}) custom-call(f32[70,8192]{1,0:T(8,128)} %col_h.1, f32[69,8192]{1,0:T(8,128)} %cpl_h.1, f32[64,128]{1,0:T(8,128)} %bitcast.2, s32[64,128]{1,0:T(8,128)} %bitcast.3, f32[9,8192]{1,0:T(8,128)} %w_h.1, ...), custom_call_target="tpu_custom_call" | custom-call | tf_op jit(solution)/shard_map/pallas_call | solution.py:353
  22.7 1.6 %shard_map.114 = (f32[70,8192]{1,0:T(8,128)}, f32[9,8192]{1,0:T(8,128)}) custom-call(f32[70,8192]{1,0:T(8,128)S(1)} %get-tuple-element.6.out, f32[64,768]{1,0:T(8,128)S(1)} %get-tuple-element.7.land, f32[9,64,128]{2,1,0:T(8,128)S(1)} %get-tuple-element.8.scaled, f32[9,64,128]{2,1,0:T(8,128)S(1)} %get-tuple-element.9.coeff_r), custom_call_target="tpu_custom_call" | custom-call | tf_op jit(solution)/shard_map/pallas_call | solution.py:381

commit v5 on v4

--- a/solution.py
+++ b/solution.py
@@ -57,7 +57,7 @@
     at_y = [(y + step) % N_Y * (2 * N_Z) for step in range(N_Y)]
     at_z = [(z + step) % N_Z * 2 for step in range(N_Z)]
     at_core = [core, 1 - core]
-    return [at_y[dy] + at_z[dz] + at_core[other] for dy, dz, other in OFFSETS]
+    return lambda dy, dz, other: at_y[dy] + at_z[dz] + at_core[other]
 
 
 def exchange(send, recv, total, sems, peers, lon, lev):
@@ -90,7 +90,7 @@
     out, land_out, scaled, coeff_r,
     col, cpl, ks, es, fs, sea_s, mask_s, w_s, co_s, ca_s, cd_s, old_s, fo_s,
     ab_send, ab_recv, to_land, from_columns,
-    ab_total, land_total, in_sem, halo_send_sem, halo_recv_sem, ab_sems, land_sems,
+    ab_total, land_total, in_sem, halo_send_sem, halo_recv_sem, ab_sems, land_sems, heard,
 ):
     lon, lev = lax.axis_index("lon"), lax.axis_index("lev")
     block = lon * N_LEV + lev
@@ -100,7 +100,7 @@
 
     own = cpl.at[:, pl.ds(LANES, COLS)]
     pairs = [
-        (co_h, co_s), (ca_h, ca_s), (cd_h, cd_s), (old_h, old_s), (fo_h, fo_s), (w_h, w_s), (cpl_h, own), (mask_h, mask_s),
+        (mask_h, mask_s), (co_h, co_s), (ca_h, ca_s), (cd_h, cd_s), (old_h, old_s), (fo_h, fo_s), (w_h, w_s), (cpl_h, own),
         (col_h, col), (sea_h, sea_s),
     ]
     loads = [pltpu.make_async_copy(src, dst, in_sem.at[n]) for n, (src, dst) in enumerate(pairs)]
@@ -111,52 +111,19 @@
 
     for one in (left_id, right_id):
         pl.semaphore_signal(barrier, inc=1, device_id=one, device_id_type=MESH)
-    peers = neighbours(lon)
-    for peer in peers:
-        pl.semaphore_signal(barrier, inc=1, device_id={"lon": peer, "lev": lev}, device_id_type=MESH)
-
-    for load in loads[:6]:
-        load.wait()
-
-    weight_sum = sum_a = sum_b = None
-    for tile in range(NT):
-        weight, coeff = row(w_s, tile), row(co_s, tile)
-        capacity, conduct = row(ca_s, tile), row(cd_s, tile)
-        held = capacity + conduct
-        inverse = 1.0 / (capacity + coeff + conduct)
-        source = capacity * row(old_s, tile) + row(fo_s, tile)
-        ratio = coeff * inverse
-        scaled[tile] = source * inverse
-        coeff_r[tile] = ratio
-        share = weight * ratio
-        weight_sum = weight if tile == 0 else weight_sum + weight
-        sum_a = share * source if tile == 0 else sum_a + share * source
-        sum_b = share * held if tile == 0 else sum_b + share * held
-    whole = 1.0 / weight_sum
-    ab_send[:, pl.ds(0, LANES)] = sum_a * whole
-    ab_send[:, pl.ds(LANES, LANES)] = sum_b * whole
-    loads[6].wait()
-    pl.semaphore_wait(barrier, N_LON + 1)
-
-    halos = [
-        pltpu.make_async_remote_copy(
-            src_ref=cpl.at[:, pl.ds(COLS, LANES)], dst_ref=cpl.at[:, pl.ds(0, LANES)],
-            send_sem=halo_send_sem.at[0], recv_sem=halo_recv_sem.at[0], device_id=right_id, device_id_type=MESH,
-        ),
-        pltpu.make_async_remote_copy(
-            src_ref=cpl.at[:, pl.ds(LANES, LANES)], dst_ref=cpl.at[:, pl.ds(COLS + LANES, LANES)],
-            send_sem=halo_send_sem.at[1], recv_sem=halo_recv_sem.at[1], device_id=left_id, device_id_type=MESH,
-        ),
-    ]
-    for halo in halos:
-        halo.start()
-    ab_out, ab_all = exchange(ab_send, ab_recv, ab_total, ab_sems, peers, lon, lev)
-    for copy in ab_out:
-        copy.start()
-    ab_recv[pl.ds(lon, 1), :] = ab_send[pl.ds(lon, 1), :]
+    at = neighbours(lon)
+    peers = [at(*offset) for offset in OFFSETS]
+    ring = [at(*offset) for offset in OFFSETS if offset[0] == 0]
+    rows_y = [at(step, 0, 0) for step in range(1, N_Y)]
+
+    def tell(semaphore, device):
+        pl.semaphore_signal(semaphore, inc=1, device_id={"lon": device, "lev": lev}, device_id_type=MESH)
+
+    for device in ring + rows_y:
+        tell(barrier, device)
 
     lane = iota((ROWS, LANES), 1)
-    loads[7].wait()
+    loads[0].wait()
     is_land = mask_s[...] == 1
     land = flag(is_land)
     running = jnp.dot(land, flag(iota((LANES, LANES), 0) <= iota((LANES, LANES), 1)), preferred_element_type=F32)
@@ -185,6 +152,44 @@
     first_slot = first_column & is_land
     last_slot = (line == (last & 63)) & (lane == (last >> 6)) & (last_flag == 1)
 
+    for load in loads[1:7]:
+        load.wait()
+
+    weight_sum = sum_a = sum_b = None
+    for tile in range(NT):
+        weight, coeff = row(w_s, tile), row(co_s, tile)
+        capacity, conduct = row(ca_s, tile), row(cd_s, tile)
+        held = capacity + conduct
+        inverse = 1.0 / (capacity + coeff + conduct)
+        source = capacity * row(old_s, tile) + row(fo_s, tile)
+        ratio = coeff * inverse
+        scaled[tile] = source * inverse
+        coeff_r[tile] = ratio
+        share = weight * ratio
+        weight_sum = weight if tile == 0 else weight_sum + weight
+        sum_a = share * source if tile == 0 else sum_a + share * source
+        sum_b = share * held if tile == 0 else sum_b + share * held
+    whole = 1.0 / weight_sum
+    ab_send[:, pl.ds(0, LANES)] = sum_a * whole
+    ab_send[:, pl.ds(LANES, LANES)] = sum_b * whole
+    loads[7].wait()
+    pl.semaphore_wait(barrier, len(ring) + len(rows_y) + 2)
+
+    halos = [
+        pltpu.make_async_remote_copy(
+            src_ref=cpl.at[:, pl.ds(COLS, LANES)], dst_ref=cpl.at[:, pl.ds(0, LANES)],
+            send_sem=halo_send_sem.at[0], recv_sem=halo_recv_sem.at[0], device_id=right_id, device_id_type=MESH,
+        ),
+        pltpu.make_async_remote_copy(
+            src_ref=cpl.at[:, pl.ds(LANES, LANES)], dst_ref=cpl.at[:, pl.ds(COLS + LANES, LANES)],
+            send_sem=halo_send_sem.at[1], recv_sem=halo_recv_sem.at[1], device_id=left_id, device_id_type=MESH,
+        ),
+    ]
+    for halo in halos:
+        halo.start()
+    for step, device in enumerate(rows_y):
+        tell(heard.at[step], device)
+
     lane_wide = iota((LEV - 1, LANES), 1)
 
     def smooth(chunk, under=0, over=2):
@@ -197,6 +202,13 @@
     smooth(ROWS - 1, over=1)
     for chunk in range(1, ROWS - 1):
         smooth(chunk)
+    for step in range(len(rows_y)):
+        pl.semaphore_wait(heard.at[step], 1)
+    ab_out, ab_all = exchange(ab_send, ab_recv, ab_total, ab_sems, peers, lon, lev)
+    for copy in ab_out:
+        copy.start()
+    ab_recv[pl.ds(lon, 1), :] = ab_send[pl.ds(lon, 1), :]
+
     def eliminate(level, carried, k_row, old_row, keep):
         k_here, offset, top, bottom = carried
         k_below = k_row(level - 1)
@@ -373,6 +385,7 @@
             pltpu.SemaphoreType.DMA((2,)),
             pltpu.SemaphoreType.DMA((2,)),
             pltpu.SemaphoreType.DMA((2,)),
+            pltpu.SemaphoreType.REGULAR((N_Y - 1,)),
         ],
         compiler_params=pltpu.CompilerParams(
             collective_id=0, has_side_effects=True, vmem_limit_bytes=24 * 2**20

time: 24.4 us -> 23.7 us (0.971)
  Pallas kernels: 23.6 us -> 23 us
    pallas_call x1, Pallas kernels: 22 us -> 21.4 us  [on_device(): pl.pallas_call(kernel, out_shape=(levels, pltpu.VMEM((ROWS, 6 * LANES), F...]
where the time goes in v5:
time: 23.7 us; the launch traced here: 23.6 us
  Pallas kernels  23 us (97%)
  between operations  0.64 us (3%)
    pallas_call x1, Pallas kernels, on_device(): pl.pallas_call(kernel, out_shape=(levels, pltpu.VMEM((ROWS, 6 * LANES), F...  21.4 us
    pallas_call x1, Pallas kernels, on_device(): pl.pallas_call(finish, out_shape=(jax.ShapeDtypeStruct((LEV, COLS), F32),...  1.59 us

profile of v5, /device:TPU:1, one launch (start us, length us, event | category | flops | bytes accessed | tf_op | source)
XLA Modules:
  0.0 23.6 jit_solution(9406043564311116781)
XLA Ops:
  0.6 21.4 %shard_map.113 = (f32[70,8192]{1,0:T(8,128)S(1)}, f32[64,768]{1,0:T(8,128)S(1)}, f32[9,64,128]{2,1,0:T(8,128)S(1)}, f32[9,64,128]{2,1,0:T(8,128)S(1)}) custom-call(f32[70,8192]{1,0:T(8,128)} %col_h.1, f32[69,8192]{1,0:T(8,128)} %cpl_h.1, f32[64,128]{1,0:T(8,128)} %bitcast.2, s32[64,128]{1,0:T(8,128)} %bitcast.3, f32[9,8192]{1,0:T(8,128)} %w_h.1, ...), custom_call_target="tpu_custom_call" | custom-call | tf_op jit(solution)/shard_map/pallas_call | solution.py:365
  22.0 1.6 %shard_map.114 = (f32[70,8192]{1,0:T(8,128)}, f32[9,8192]{1,0:T(8,128)}) custom-call(f32[70,8192]{1,0:T(8,128)S(1)} %get-tuple-element.6.out, f32[64,768]{1,0:T(8,128)S(1)} %get-tuple-element.7.land, f32[9,64,128]{2,1,0:T(8,128)S(1)} %get-tuple-element.8.scaled, f32[9,64,128]{2,1,0:T(8,128)S(1)} %get-tuple-element.9.coeff_r), custom_call_target="tpu_custom_call" | custom-call | tf_op jit(solution)/shard_map/pallas_call | solution.py:394

commit v6 on v5

--- a/solution.py
+++ b/solution.py
@@ -90,7 +90,7 @@
     out, land_out, scaled, coeff_r,
     col, cpl, ks, es, fs, sea_s, mask_s, w_s, co_s, ca_s, cd_s, old_s, fo_s,
     ab_send, ab_recv, to_land, from_columns,
-    ab_total, land_total, in_sem, halo_send_sem, halo_recv_sem, ab_sems, land_sems, heard,
+    halo_out, halo_in, ab_total, land_total, in_sem, halo_send_sem, halo_recv_sem, ab_sems, land_sems, heard,
 ):
     lon, lev = lax.axis_index("lon"), lax.axis_index("lev")
     block = lon * N_LEV + lev
@@ -98,9 +98,8 @@
     right_id = {"lon": right // N_LEV, "lev": right % N_LEV}
     left_id = {"lon": left // N_LEV, "lev": left % N_LEV}
 
-    own = cpl.at[:, pl.ds(LANES, COLS)]
     pairs = [
-        (mask_h, mask_s), (co_h, co_s), (ca_h, ca_s), (cd_h, cd_s), (old_h, old_s), (fo_h, fo_s), (w_h, w_s), (cpl_h, own),
+        (mask_h, mask_s), (co_h, co_s), (ca_h, ca_s), (cd_h, cd_s), (old_h, old_s), (fo_h, fo_s), (w_h, w_s), (cpl_h, cpl),
         (col_h, col), (sea_h, sea_s),
     ]
     loads = [pltpu.make_async_copy(src, dst, in_sem.at[n]) for n, (src, dst) in enumerate(pairs)]
@@ -113,7 +112,7 @@
         pl.semaphore_signal(barrier, inc=1, device_id=one, device_id_type=MESH)
     at = neighbours(lon)
     peers = [at(*offset) for offset in OFFSETS]
-    ring = [at(*offset) for offset in OFFSETS if offset[0] == 0]
+    ring = [at(*offset) for offset in OFFSETS if offset[0] == 0 and away(offset[1], N_Z) < N_Z // 2]
     rows_y = [at(step, 0, 0) for step in range(1, N_Y)]
 
     def tell(semaphore, device):
@@ -173,40 +172,59 @@
     ab_send[:, pl.ds(0, LANES)] = sum_a * whole
     ab_send[:, pl.ds(LANES, LANES)] = sum_b * whole
     loads[7].wait()
+
+    lane_wide = iota((LEV - 1, LANES), 1)
+    diagonal = iota((LEV - 1, LANES), 0) == lane_wide
+
+    def as_row(column):
+        wide = jnp.broadcast_to(column, (LEV - 1, LANES))
+        return jnp.sum(jnp.where(diagonal, wide, 0.0), axis=0, keepdims=True)
+
+    def as_column(line):
+        wide = jnp.broadcast_to(line, (LEV - 1, LANES))
+        return jnp.sum(jnp.where(diagonal, wide, 0.0), axis=1, keepdims=True)
+
+    halo_out[pl.ds(0, 1), :] = as_row(cpl[:, pl.ds(COLS - LANES, LANES)][:, LANES - 1 :])
+    halo_out[pl.ds(8, 1), :] = as_row(cpl[:, pl.ds(0, LANES)][:, :1])
     pl.semaphore_wait(barrier, len(ring) + len(rows_y) + 2)
 
     halos = [
         pltpu.make_async_remote_copy(
-            src_ref=cpl.at[:, pl.ds(COLS, LANES)], dst_ref=cpl.at[:, pl.ds(0, LANES)],
-            send_sem=halo_send_sem.at[0], recv_sem=halo_recv_sem.at[0], device_id=right_id, device_id_type=MESH,
-        ),
-        pltpu.make_async_remote_copy(
-            src_ref=cpl.at[:, pl.ds(LANES, LANES)], dst_ref=cpl.at[:, pl.ds(COLS + LANES, LANES)],
-            send_sem=halo_send_sem.at[1], recv_sem=halo_recv_sem.at[1], device_id=left_id, device_id_type=MESH,
-        ),
+            src_ref=halo_out.at[pl.ds(line, 1), :], dst_ref=halo_in.at[pl.ds(line, 1), :],
+            send_sem=halo_send_sem.at[n], recv_sem=halo_recv_sem.at[n], device_id=device, device_id_type=MESH,
+        )
+        for n, (line, device) in enumerate(((0, right_id), (8, left_id)))
     ]
     for halo in halos:
         halo.start()
     for step, device in enumerate(rows_y):
-        tell(heard.at[step], device)
-
-    lane_wide = iota((LEV - 1, LANES), 1)
-
-    def smooth(chunk, under=0, over=2):
-        below, centre, above = (cpl[:, pl.ds((chunk + n) * LANES, LANES)] for n in (under, 1, over))
-        low = pltpu.roll(jnp.where(lane_wide == LANES - 1, below, centre), 1, 1)
-        high = pltpu.roll(jnp.where(lane_wide == 0, above, centre), LANES - 1, 1)
+        tell(heard.at[1 + step], device)
+
+    def smooth(chunk, left=None, right=None):
+        centre = cpl[:, pl.ds(chunk * LANES, LANES)]
+        if left is None:
+            below = cpl[:, pl.ds((chunk - 1) * LANES, LANES)]
+            low = pltpu.roll(jnp.where(lane_wide == LANES - 1, below, centre), 1, 1)
+        else:
+            low = jnp.where(lane_wide == 0, left, pltpu.roll(centre, 1, 1))
+        if right is None:
+            above = cpl[:, pl.ds((chunk + 1) * LANES, LANES)]
+            high = pltpu.roll(jnp.where(lane_wide == 0, above, centre), LANES - 1, 1)
+        else:
+            high = jnp.where(lane_wide == LANES - 1, right, pltpu.roll(centre, LANES - 1, 1))
         ks[:, pl.ds(chunk * LANES, LANES)] = (low + 2.0 * centre + high) * 0.25
 
-    smooth(0, under=1)
-    smooth(ROWS - 1, over=1)
+    smooth(0, left=0.0)
+    smooth(ROWS - 1, right=0.0)
     for chunk in range(1, ROWS - 1):
         smooth(chunk)
     for step in range(len(rows_y)):
-        pl.semaphore_wait(heard.at[step], 1)
+        pl.semaphore_wait(heard.at[1 + step], 1)
+    tell(heard.at[0], at(0, N_Z - 1, 0))
     ab_out, ab_all = exchange(ab_send, ab_recv, ab_total, ab_sems, peers, lon, lev)
-    for copy in ab_out:
-        copy.start()
+    for offset, copy in zip(OFFSETS, ab_out):
+        if offset[1] != N_Z // 2:
+            copy.start()
     ab_recv[pl.ds(lon, 1), :] = ab_send[pl.ds(lon, 1), :]
 
     def eliminate(level, carried, k_row, old_row, keep):
@@ -241,6 +259,11 @@
     loads[8].wait()
     k_second, offset_two, pivot_base, _ = lax.fori_loop(0, (LEV - 2) // 4, all_columns, start_of((ROWS, LANES)))
     fields = [row(ks, 0), pivot_base, row(col, 1) + k_second * offset_two, row(col, 0)]
+
+    pl.semaphore_wait(heard.at[0], 1)
+    for offset, copy in zip(OFFSETS, ab_out):
+        if offset[1] == N_Z // 2:
+            copy.start()
 
     targets = jnp.concatenate(
         [
@@ -267,8 +290,8 @@
 
     for halo in halos:
         halo.wait_recv()
-    smooth(0)
-    smooth(ROWS - 1)
+    smooth(0, left=as_column(halo_in[pl.ds(0, 1), :]))
+    smooth(ROWS - 1, right=as_column(halo_in[pl.ds(8, 1), :]))
     sublane = iota((8, LANES), 0)
 
     def edge_row(ref, level):
@@ -369,7 +392,7 @@
         out_specs=(in_vmem,) * 4,
         scratch_shapes=[
             levels,
-            pltpu.VMEM((LEV - 1, COLS + 2 * LANES), F32),
+            pltpu.VMEM((LEV - 1, COLS), F32),
             pltpu.VMEM((LEV - 1, COLS), F32),
             pltpu.VMEM((LEV, ROWS, LANES), F32),
             pltpu.VMEM((LEV, ROWS, LANES), F32),
@@ -378,6 +401,7 @@
             *[tile_rows] * 6,
             *[pltpu.VMEM((N_LON, 2 * LANES), F32)] * 2,
             *[pltpu.VMEM((N_LON, 4 * LANES), F32)] * 2,
+            *[pltpu.VMEM((16, LANES), F32)] * 2,
             pltpu.VMEM(((N_LON - 1) * 2, LANES), F32),
             pltpu.VMEM(((N_LON - 1) * 4, LANES), F32),
             pltpu.SemaphoreType.DMA((10,)),
@@ -385,7 +409,7 @@
             pltpu.SemaphoreType.DMA((2,)),
             pltpu.SemaphoreType.DMA((2,)),
             pltpu.SemaphoreType.DMA((2,)),
-            pltpu.SemaphoreType.REGULAR((N_Y - 1,)),
+            pltpu.SemaphoreType.REGULAR((N_Y,)),
         ],
         compiler_params=pltpu.CompilerParams(
             collective_id=0, has_side_effects=True, vmem_limit_bytes=24 * 2**20

time: 23.7 us -> 23.3 us (0.983)
  Pallas kernels: 23 us -> 22.6 us
    pallas_call x1, Pallas kernels: 21.4 us -> 21 us  [on_device(): pl.pallas_call(kernel, out_shape=(levels, pltpu.VMEM((ROWS, 6 * LANES), F...]
where the time goes in v6:
time: 23.3 us
  Pallas kernels  22.6 us (97%)
  between operations  0.64 us (3%)
    pallas_call x1, Pallas kernels, on_device(): pl.pallas_call(kernel, out_shape=(levels, pltpu.VMEM((ROWS, 6 * LANES), F...  21 us
    pallas_call x1, Pallas kernels, on_device(): pl.pallas_call(finish, out_shape=(jax.ShapeDtypeStruct((LEV, COLS), F32),...  1.59 us

profile of v6, /device:TPU:1, one launch (start us, length us, event | category | flops | bytes accessed | tf_op | source)
XLA Modules:
  0.0 23.3 jit_solution(6448858148269246612)
XLA Ops:
  0.6 21.0 %shard_map.113 = (f32[70,8192]{1,0:T(8,128)S(1)}, f32[64,768]{1,0:T(8,128)S(1)}, f32[9,64,128]{2,1,0:T(8,128)S(1)}, f32[9,64,128]{2,1,0:T(8,128)S(1)}) custom-call(f32[70,8192]{1,0:T(8,128)} %col_h.1, f32[69,8192]{1,0:T(8,128)} %cpl_h.1, f32[64,128]{1,0:T(8,128)} %bitcast.2, s32[64,128]{1,0:T(8,128)} %bitcast.3, f32[9,8192]{1,0:T(8,128)} %w_h.1, ...), custom_call_target="tpu_custom_call" | custom-call | tf_op jit(solution)/shard_map/pallas_call | solution.py:388
  21.7 1.6 %shard_map.114 = (f32[70,8192]{1,0:T(8,128)}, f32[9,8192]{1,0:T(8,128)}) custom-call(f32[70,8192]{1,0:T(8,128)S(1)} %get-tuple-element.6.out, f32[64,768]{1,0:T(8,128)S(1)} %get-tuple-element.7.land, f32[9,64,128]{2,1,0:T(8,128)S(1)} %get-tuple-element.8.scaled, f32[9,64,128]{2,1,0:T(8,128)S(1)} %get-tuple-element.9.coeff_r), custom_call_target="tpu_custom_call" | custom-call | tf_op jit(solution)/shard_map/pallas_call | solution.py:418

commit v7 on v6

--- a/solution.py
+++ b/solution.py
@@ -90,7 +90,7 @@
     out, land_out, scaled, coeff_r,
     col, cpl, ks, es, fs, sea_s, mask_s, w_s, co_s, ca_s, cd_s, old_s, fo_s,
     ab_send, ab_recv, to_land, from_columns,
-    halo_out, halo_in, ab_total, land_total, in_sem, halo_send_sem, halo_recv_sem, ab_sems, land_sems, heard,
+    halo_out, halo_in, missing, ab_total, land_total, in_sem, halo_send_sem, halo_recv_sem, ab_sems, land_sems, heard,
 ):
     lon, lev = lax.axis_index("lon"), lax.axis_index("lev")
     block = lon * N_LEV + lev
@@ -102,10 +102,6 @@
         (mask_h, mask_s), (co_h, co_s), (ca_h, ca_s), (cd_h, cd_s), (old_h, old_s), (fo_h, fo_s), (w_h, w_s), (cpl_h, cpl),
         (col_h, col), (sea_h, sea_s),
     ]
-    loads = [pltpu.make_async_copy(src, dst, in_sem.at[n]) for n, (src, dst) in enumerate(pairs)]
-    for load in loads:
-        load.start()
-
     barrier = pltpu.get_barrier_semaphore()
 
     for one in (left_id, right_id):
@@ -120,6 +116,10 @@
 
     for device in ring + rows_y:
         tell(barrier, device)
+
+    loads = [pltpu.make_async_copy(src, dst, in_sem.at[n]) for n, (src, dst) in enumerate(pairs)]
+    for load in loads:
+        load.start()
 
     lane = iota((ROWS, LANES), 1)
     loads[0].wait()
@@ -290,13 +290,19 @@
 
     for halo in halos:
         halo.wait_recv()
-    smooth(0, left=as_column(halo_in[pl.ds(0, 1), :]))
-    smooth(ROWS - 1, right=as_column(halo_in[pl.ds(8, 1), :]))
-    sublane = iota((8, LANES), 0)
+    missing[...] = 0.25 * jnp.where(
+        lane_wide == 0, as_column(halo_in[pl.ds(0, 1), :]),
+        jnp.where(lane_wide == LANES - 1, as_column(halo_in[pl.ds(8, 1), :]), 0.0),
+    )
+    sublane, edge_lane = iota((8, LANES), 0), iota((8, LANES), 1)
+    corners = ((sublane == 0) & (edge_lane == 0)) | ((sublane == 7) & (edge_lane == LANES - 1))
 
     def edge_row(ref, level):
         low, high = (ref[pl.ds(level, 1), pl.ds(start, 8 * LANES)].reshape(8, LANES) for start in (0, COLS - 8 * LANES))
         return jnp.where(sublane == 0, low, high)
+
+    def edge_smooth(level):
+        return edge_row(ks, level) + jnp.where(corners, missing[pl.ds(level, 1), :], 0.0)
 
     def keep_edges(level, offset, factor):
         for ref, value in ((es, offset), (fs, factor)):
@@ -306,11 +312,11 @@
     edge = start_of((8, LANES))
     for level in range(LEV - 1, 1, -1):
         edge, inverse = eliminate(
-            level, edge, lambda level: edge_row(ks, level), lambda level: edge_row(col, level), keep_edges
+            level, edge, edge_smooth, lambda level: edge_row(col, level), keep_edges
         )
         if level % 12 == 2:
             edge = scaled_down(edge, inverse)
-    edge_fields = [edge_row(ks, 0), edge[2], edge_row(col, 1) + edge[0] * edge[1], edge_row(col, 0)]
+    edge_fields = [edge_smooth(0), edge[2], edge_row(col, 1) + edge[0] * edge[1], edge_row(col, 0)]
 
     for n, value in enumerate(edge_fields):
         part = pl.ds(n * LANES, LANES)
@@ -402,6 +408,7 @@
             *[pltpu.VMEM((N_LON, 2 * LANES), F32)] * 2,
             *[pltpu.VMEM((N_LON, 4 * LANES), F32)] * 2,
             *[pltpu.VMEM((16, LANES), F32)] * 2,
+            pltpu.VMEM((LEV - 1, LANES), F32),
             pltpu.VMEM(((N_LON - 1) * 2, LANES), F32),
             pltpu.VMEM(((N_LON - 1) * 4, LANES), F32),
             pltpu.SemaphoreType.DMA((10,)),

time: 23.3 us -> 23.3 us (level)
  no operation moved by 1% of the time
where the time goes in v7:
time: 23.3 us
  Pallas kernels  22.6 us (97%)
  between operations  0.64 us (3%)
    pallas_call x1, Pallas kernels, on_device(): pl.pallas_call(kernel, out_shape=(levels, pltpu.VMEM((ROWS, 6 * LANES), F...  21 us
    pallas_call x1, Pallas kernels, on_device(): pl.pallas_call(finish, out_shape=(jax.ShapeDtypeStruct((LEV, COLS), F32),...  1.59 us

profile of v7, /device:TPU:1, one launch (start us, length us, event | category | flops | bytes accessed | tf_op | source)
XLA Modules:
  0.0 23.3 jit_solution(1637499069689099094)
XLA Ops:
  0.6 21.0 %shard_map.113 = (f32[70,8192]{1,0:T(8,128)S(1)}, f32[64,768]{1,0:T(8,128)S(1)}, f32[9,64,128]{2,1,0:T(8,128)S(1)}, f32[9,64,128]{2,1,0:T(8,128)S(1)}) custom-call(f32[70,8192]{1,0:T(8,128)} %col_h.1, f32[69,8192]{1,0:T(8,128)} %cpl_h.1, f32[64,128]{1,0:T(8,128)} %bitcast.2, s32[64,128]{1,0:T(8,128)} %bitcast.3, f32[9,8192]{1,0:T(8,128)} %w_h.1, ...), custom_call_target="tpu_custom_call" | custom-call | tf_op jit(solution)/shard_map/pallas_call | solution.py:394
  21.7 1.6 %shard_map.114 = (f32[70,8192]{1,0:T(8,128)}, f32[9,8192]{1,0:T(8,128)}) custom-call(f32[70,8192]{1,0:T(8,128)S(1)} %get-tuple-element.6.out, f32[64,768]{1,0:T(8,128)S(1)} %get-tuple-element.7.land, f32[9,64,128]{2,1,0:T(8,128)S(1)} %get-tuple-element.8.scaled, f32[9,64,128]{2,1,0:T(8,128)S(1)} %get-tuple-element.9.coeff_r), custom_call_target="tpu_custom_call" | custom-call | tf_op jit(solution)/shard_map/pallas_call | solution.py:425
